TPU v7x, 8 devices: a whole 2x2x1 slice. The times are simulated.
8 devices in a mesh: dp: 1 (over z), fsdp: 2 (over y), ep: 4 (over x, core).
Axes of the slice: x: 2, y: 2, z: 1, core: 2. Of those that a mesh axis runs over, the one named last changes fastest.
Arguments:
- hidden: bfloat16 [16384, 2304], P(('dp', 'fsdp', 'ep'))
- norm_gain: bfloat16 [2304], replicated
- w_router: bfloat16 [2304, 8], replicated
- w_gate: bfloat16 [8, 2304, 5760], P('ep', 'fsdp')
- w_up: bfloat16 [8, 2304, 5760], P('ep', 'fsdp')
- w_down: bfloat16 [8, 5760, 2304], P('ep', None, 'fsdp')
- top2_ids: int32 [16384, 2], P(('dp', 'fsdp', 'ep'))
Outputs:
- output: bfloat16 [16384, 2304], P(('dp', 'fsdp', 'ep'))
All inputs are finite; a program needn't handle non-finite values.
Results may differ from a plain program's by a relative error of at most 0.001.
Values are sent between devices in bfloat16 or wider.
A program may use at most 1 GiB of HBM per device.

v0:
```python
import jax
import jax.numpy as jnp
from jax import lax
from jax.sharding import PartitionSpec as P

EPS = 1e-5


def norm_and_gates(hidden, norm_gain, w_router, top2_ids):
    hidden_f32 = hidden.astype(jnp.float32)
    mean_sq = jnp.mean(hidden_f32 * hidden_f32, axis=-1, keepdims=True)
    normed = (hidden_f32 * lax.rsqrt(mean_sq + EPS) * norm_gain.astype(jnp.float32)).astype(jnp.bfloat16)
    logits = jnp.dot(normed, w_router, preferred_element_type=jnp.float32)
    gate_probs = jax.nn.softmax(jnp.take_along_axis(logits, top2_ids, axis=1), axis=-1)
    return hidden_f32, normed, gate_probs


def route_slots(top2_ids, num_experts, capacity):
    flat_ids = top2_ids.reshape(-1)
    onehot = (flat_ids[:, None] == jnp.arange(num_experts, dtype=jnp.int32)[None, :]).astype(jnp.int32)
    position = jnp.sum((jnp.cumsum(onehot, axis=0) - 1) * onehot, axis=1)
    slot_ids = jnp.where(position < capacity, flat_ids * capacity + position, num_experts * capacity)
    return slot_ids.reshape(top2_ids.shape)


def gather_rows(normed, slot_ids, num_slots):
    tok_count = slot_ids.shape[0]
    token_index = jnp.broadcast_to(jnp.arange(tok_count, dtype=jnp.int32)[:, None], slot_ids.shape)
    source = jnp.full((num_slots,), tok_count, dtype=jnp.int32).at[slot_ids.reshape(-1)].set(token_index.reshape(-1), mode='drop')
    return jnp.take(normed, source, axis=0, mode='fill', fill_value=0)


def take_slots(expert_rows, slot_ids):
    return jnp.take(expert_rows, slot_ids, axis=0, mode='fill', fill_value=0)


def expert_block(rows_in, gate_full, up_full, down_full):
    act_a = jnp.einsum('ecd,edf->ecf', rows_in, gate_full, preferred_element_type=jnp.float32)
    act_b = jnp.einsum('ecd,edf->ecf', rows_in, up_full, preferred_element_type=jnp.float32)
    hidden_act = (jax.nn.silu(act_a) * act_b).astype(jnp.bfloat16)
    return jnp.einsum('ecf,efd->ecd', hidden_act, down_full, preferred_element_type=jnp.float32).astype(jnp.bfloat16)


def local_block(hidden, norm_gain, w_router, w_gate, w_up, w_down, top2_ids):
    tok_local, d_model = hidden.shape
    num_experts = w_router.shape[1]
    capacity = (5 * tok_local + 2 * num_experts - 1) // (2 * num_experts)
    hidden_f32, normed, gate_probs = norm_and_gates(hidden, norm_gain, w_router, top2_ids)
    slot_ids = route_slots(top2_ids, num_experts, capacity)
    send_rows = gather_rows(normed, slot_ids, num_experts * capacity).reshape(num_experts, capacity, d_model)
    gate_full = lax.all_gather(w_gate, 'fsdp', axis=1, tiled=True)
    up_full = lax.all_gather(w_up, 'fsdp', axis=1, tiled=True)
    down_full = lax.all_gather(w_down, 'fsdp', axis=2, tiled=True)
    recv_rows = lax.all_to_all(send_rows, 'ep', 0, 1, tiled=True)
    expert_out = expert_block(recv_rows, gate_full, up_full, down_full)
    back_rows = lax.all_to_all(expert_out, 'ep', 1, 0, tiled=True)
    returned = take_slots(back_rows.reshape(num_experts * capacity, d_model), slot_ids)
    moe_sum = jnp.sum(gate_probs[:, :, None] * returned.astype(jnp.float32), axis=1)
    return (hidden_f32 + moe_sum).astype(jnp.bfloat16)


def solution(mesh):
    tok_spec = P(('dp', 'fsdp', 'ep'), None)
    in_specs = (tok_spec, P(None), P(None, None), P('ep', 'fsdp', None), P('ep', 'fsdp', None), P('ep', None, 'fsdp'), tok_spec)
    return jax.shard_map(local_block, mesh=mesh, in_specs=in_specs, out_specs=tok_spec, check_vma=False)
```

profile of v0, /device:TPU:1, one launch (start us, length us, event | category | flops | bytes accessed | tf_op | source)
XLA Modules:
  0.0 2615.2 jit_solution(7508500534556635956)
XLA Ops:
  6.5 0.7 all-gather.6.cloned.1.call-update
  7.3 0.7 all-gather.4.cloned.1.call-update
  8.0 0.4 copy.35
  8.4 0.5 eq.29
  8.9 0.5 eq.25
  9.4 2.3 reduce-window.6
  11.7 0.3 slice_reduce_fusion
  12.0 0.2 reduce-window.9
  12.2 0.4 copy.40
  12.6 0.6 mul.59
  13.3 0.5 reshape.148
  14.0 0.5 copy-done.4
  14.6 15.5 scatter_custom_fusion
  30.2 5.6 fusion.2
  35.8 9.7 fusion.4
  45.4 48.5 %gather_fusion = bf16[5120,2304]{1,0:T(8,128)(2,1)} fusion(bf16[2048,2304]{1,0:T(8,128)(2,1)} %fusion.4, s32[5120]{0:T(1024)S(1)} %fusion.9), kind=kCustom, calls=%fused_computation | custom fusion | bytes 47206400 | tf_op jit(solution)/shard_map/jit(_take)/gather | solution.py:30
  93.9 20.2 broadcast_select_fusion.1
  114.2 8.7 all-to-all-start
  122.9 0.7 all-gather.8.cloned.1.call-update
  123.6 254.5 %all-to-all-done = bf16[8,640,2304]{2,1,0:T(8,128)(2,1)} async-done(((bf16[8,640,2304]{2,1,0:T(8,128)(2,1)}), bf16[8,640,2304]{2,1,0:T(8,128)(2,1)}, u32[]{:S(2)}, u32[]{:S(2)}) %all-to-all-start) | async-done | bytes 23592992 | tf_op jit(solution)/shard_map/all_to_all | solution.py:54
  378.0 19.8 copy.41
  397.8 221.6 %all-gather.6.cloned.1.call-done = bf16[2,2304,5760]{2,1,0:T(8,128)(2,1)} async-done(((bf16[2,1152,5760]{2,1,0:T(8,128)(2,1)}), bf16[2,2304,5760]{2,1,0:T(8,128)(2,1)}) %all-gather.6.cloned.1.call-update) | async-done | bytes 53084176 | tf_op jit(solution)/shard_map/all_gather | solution.py:52
  619.5 157.9 %fusion.19 = f32[2,2560,5760]{2,1,0:T(8,128)} fusion(bf16[2,2560,2304]{2,1,0:T(8,128)(2,1)} %bitcast.47, bf16[2,2304,5760]{2,1,0:T(8,128)(2,1)} %all-gather.6.cloned.1.call-done), kind=kOutput, calls=%fused_computation.48 | convolution fusion | flops 135895449600 | bytes 194641920 | tf_op jit(solution)/shard_map/ecd,edf->ecf/dot_general | solution.py:39
  777.4 452.7 %all-gather.4.cloned.1.call-done = bf16[2,2304,5760]{2,1,0:T(8,128)(2,1)} async-done(((bf16[2,1152,5760]{2,1,0:T(8,128)(2,1)}), bf16[2,2304,5760]{2,1,0:T(8,128)(2,1)}) %all-gather.4.cloned.1.call-update) | async-done | bytes 53084176 | tf_op jit(solution)/shard_map/all_gather | solution.py:51
  1230.1 180.4 %multiply_convert_fusion.6 = bf16[2,2560,5760]{2,1,0:T(8,128)(2,1)} fusion(f32[2,2560,5760]{2,1,0:T(8,128)} %fusion.19, bf16[2,2560,2304]{2,1,0:T(8,128)(2,1)} %bitcast.48, bf16[2,2304,5760]{2,1,0:T(8,128)(2,1)} %all-gather.4.cloned.1.call-done), kind=kOutput, calls=%fused_computation.4.clone.clone.clone.clone.1 | convolution fusion | flops 136072396800 | bytes 253624320 | tf_op jit(solution)/shard_map/ecd,edf->ecf/dot_general | solution.py:38
  1410.4 427.9 %all-gather.8.cloned.1.call-done = bf16[2,5760,2304]{2,1,0:T(8,128)(2,1)} async-done(((bf16[2,5760,1152]{2,1,0:T(8,128)(2,1)}), bf16[2,5760,2304]{2,1,0:T(8,128)(2,1)}) %all-gather.8.cloned.1.call-update) | async-done | bytes 53084176 | tf_op jit(solution)/shard_map/all_gather | solution.py:53
  1838.4 152.4 %fusion.1 = bf16[2,2560,2304]{2,1,0:T(8,128)(2,1)} fusion(bf16[2,5760,2304]{2,1,0:T(8,128)(2,1)} %all-gather.8.cloned.1.call-done, bf16[2,2560,5760]{2,1,0:T(8,128)(2,1)} %multiply_convert_fusion.6), kind=kOutput, calls=%fused_computation.11 | convolution fusion | flops 135907246080 | bytes 135659520 | tf_op jit(solution)/shard_map/ecf,efd->ecd/dot_general | solution.py:41
  1990.8 43.0 %copy.42 = bf16[2,2560,2304]{2,0,1:T(2,128)(2,1)} copy(bf16[2,2560,2304]{2,1,0:T(8,128)(2,1)} %fusion.1) | data formatting | bytes 47185920 | tf_op jit(solution)/shard_map/convert_element_type | solution.py:41
  2033.8 9.4 all-to-all-start.1
  2043.2 1.0 reduce_sum.43
  2044.2 0.3 copy.37
  2044.5 0.6 compare_and_fusion
  2045.2 0.4 copy.44
  2045.6 1.1 reshape.132
  2046.7 0.4 copy.32
  2047.0 0.5 reshape.138
  2047.5 6.2 fusion.18
  2053.7 24.5 gather_fusion.2
  2078.3 1.0 reshape.141
  2079.3 0.3 copy.33
  2079.7 0.4 copy.34
  2080.1 0.5 copy.39
  2080.6 217.4 %all-to-all-done.1 = bf16[2,2560,2304]{2,0,1:T(2,128)(2,1)} async-done(((bf16[2,2560,2304]{2,0,1:T(2,128)(2,1)}), bf16[2,2560,2304]{2,0,1:T(2,128)(2,1)}, u32[]{:S(2)}, u32[]{:S(2)}) %all-to-all-start.1) | async-done | bytes 23592992 | tf_op jit(solution)/shard_map/all_to_all | solution.py:56
  2298.1 22.5 copy.43
  2320.6 45.9 %gather_fusion.1 = bf16[4096,2304]{1,0:T(8,128)(2,1)} fusion(bf16[5120,2304]{1,0:T(8,128)(2,1)} %bitcast.45, s32[4096]{0:T(1024)S(1)} %broadcast_clamp_fusion), kind=kCustom, calls=%fused_computation.1 | custom fusion | bytes 37765120 | tf_op jit(solution)/shard_map/jit(_take)/gather | solution.py:34
  2366.5 36.6 %reshape.131 = bf16[2048,2,2304]{2,1,0:T(2,128)(2,1)} reshape(bf16[4096,2304]{1,0:T(8,128)(2,1)} %gather_fusion.1) | data formatting | bytes 37748736 | tf_op jit(solution)/shard_map/jit(_take)/gather | solution.py:34
  2403.1 195.3 %multiply_reduce_fusion = f32[2048,2304]{1,0:T(8,128)S(1)} fusion(bf16[2048,2,2304]{2,1,0:T(2,128)(2,1)} %reshape.131, pred[2048,2]{1,0:T(8,128)(4,1)S(1)} %copy.39, f32[2048,2]{1,0:T(8,128)S(1)} %copy.34), kind=kLoop, calls=%fused_computation.6 | loop fusion | flops 33030144 | bytes 37769216 | tf_op jit(solution)/shard_map/reduce_sum | solution.py:58
  2598.4 9.9 fusion.5
  (36 shorter events, 0.7 us)
Async XLA Ops:
  6.5 2041.0 %copy-start = (bf16[2304,8]{0,1:T(8,128)(2,1)S(1)}, bf16[2304,8]{0,1:T(8,128)(2,1)}, u32[]{:S(2)}) copy-start(bf16[2304,8]{0,1:T(8,128)(2,1)} %param.9) | copy-start | bytes 110596
  6.5 1.5 copy-start.1
  6.5 613.0 %all-gather.6.cloned.1.call-start = ((), (), s32[]{:S(2)}) async-start(), calls=%async_computation.3 | async-start | bytes 79626240 | tf_op jit(solution)/shard_map/all_gather | solution.py:52
  7.3 6.5 copy-start.8
  7.3 1222.8 %all-gather.4.cloned.1.call-start = ((), (), s32[]{:S(2)}) async-start(), calls=%async_computation.2 | async-start | bytes 79626240 | tf_op jit(solution)/shard_map/all_gather | solution.py:51
  14.0 0.6 copy-start.4
  114.2 263.9 %all-to-all-start = ((bf16[8,640,2304]{2,1,0:T(8,128)(2,1)}), bf16[8,640,2304]{2,1,0:T(8,128)(2,1)}, u32[]{:S(2)}, u32[]{:S(2)}) async-start(bf16[8,640,2304]{2,1,0:T(8,128)(2,1)} %broadcast_select_fusion.1), calls=%async_computation | async-start | bytes 47185920 | tf_op jit(solution)/shard_map/all_to_all | solution.py:54
  122.8 1715.6 %all-gather.8.cloned.1.call-start = ((), (), s32[]{:S(2)}) async-start(), calls=%async_computation.4 | async-start | bytes 79626240 | tf_op jit(solution)/shard_map/all_gather | solution.py:53
  2033.8 9.4 copy-start.5
  2033.8 10.8 copy-start.2
  2033.8 264.3 %all-to-all-start.1 = ((bf16[2,2560,2304]{2,0,1:T(2,128)(2,1)}), bf16[2,2560,2304]{2,0,1:T(2,128)(2,1)}, u32[]{:S(2)}, u32[]{:S(2)}) async-start(bf16[2,2560,2304]{2,0,1:T(2,128)(2,1)} %copy.42), calls=%async_computation.1 | async-start | bytes 47185920 | tf_op jit(solution)/shard_map/all_to_all | solution.py:56
  2053.7 25.9 copy-start.3
  2053.7 26.4 %copy-start.7 = (pred[2048,2]{0,1:T(4,128)(4,1)S(1)}, pred[2048,2]{0,1:T(4,128)(4,1)}, u32[]{:S(2)}) copy-start(pred[2048,2]{0,1:T(4,128)(4,1)} %get-tuple-element.7) | copy-start | bytes 12292
  2053.7 26.9 %copy-start.6 = (s32[4096]{0:T(1024)S(1)}, s32[4096]{0:T(1024)}, u32[]{:S(2)}) copy-start(s32[4096]{0:T(1024)} %reshape.132) | copy-start | bytes 49156
Sparse Core Ops, SparseCore 0:
  8.9 610.5 all-gather.5
  621.0 609.0 all-gather.3
  1231.6 606.7 all-gather.7
where the time goes:
time: 2630 us; the launch traced here: 2620 us
  waiting for transfers between devices  1580 us (60%)
  matrix products  497 us (19%)
  local copies, waits for them, and re-layouts  266 us (10%)
  other arithmetic  244 us (9%)
    all_gather x1, waiting for transfers between devices, local_block(): gate_full = lax.all_gather(w_gate, 'fsdp', axis=1, tiled=True)  453 us
    all_gather x1, waiting for transfers between devices, local_block(): down_full = lax.all_gather(w_down, 'fsdp', axis=2, tiled=True)  428 us
    all_to_all x1, waiting for transfers between devices, local_block(): recv_rows = lax.all_to_all(send_rows, 'ep', 0, 1, tiled=True)  254 us
    all_gather x1, waiting for transfers between devices, local_block(): up_full = lax.all_gather(w_up, 'fsdp', axis=1, tiled=True)  222 us
    all_to_all x1, waiting for transfers between devices, local_block(): back_rows = lax.all_to_all(expert_out, 'ep', 1, 0, tiled=True)  217 us
    reduce_sum x1, other arithmetic, local_block(): jnp.sum(gate_probs[:, :, None] * returned.astype(jnp.float32), axis=1)  195 us
    dot_general x1, matrix products, expert_block(): jnp.einsum('ecd,edf->ecf', rows_in, gate_full, preferred_element_type=jnp...  180 us
    dot_general x1, matrix products, expert_block(): jnp.einsum('ecd,edf->ecf', rows_in, up_full, preferred_element_type=jnp.f...  158 us
  transfers between devices with their start and end apart: 5, of which 5 were waited for; matrix products, arithmetic and copies ran while one was open for 19% of the time, Pallas kernels for 0%

commit v1 on v0

v1 whole, which is shorter than its diff:
```python
import functools

import jax
import jax.numpy as jnp
from jax import lax
from jax.experimental import pallas as pl
from jax.experimental.pallas import tpu as pltpu
from jax.sharding import PartitionSpec as P

EPS = 1e-5
MESH = pl.DeviceIdType.MESH
ANY = pl.BlockSpec(memory_space=pl.ANY)
VMEM = pl.BlockSpec(memory_space=pltpu.VMEM)
F32 = jnp.float32
BF16 = jnp.bfloat16
FF_CHUNKS = 5
HALF_CHUNKS = 3


def routes(top2_ids, num_experts, capacity):
    tok = top2_ids.shape[0]
    place = (top2_ids % 2) * (num_experts // 2) + top2_ids // 2
    choice = place[:, :, None] == jnp.arange(num_experts, dtype=jnp.int32)
    chosen = jnp.any(choice, axis=1)
    step = jnp.arange(tok, dtype=jnp.int32)
    before = (step[:, None] > step[None, :]).astype(BF16)
    position = jnp.dot(before, chosen.astype(BF16), preferred_element_type=F32).astype(jnp.int32)
    kept = jnp.where(chosen & (position < capacity), position, -1)
    base = jnp.arange(num_experts, dtype=jnp.int32) * capacity
    flat = jnp.where(kept >= 0, kept + base, -1)
    slots = jnp.sum(jnp.where(choice, flat[:, None, :], 0), axis=2)
    return kept.T, slots


def moe_kernel(cap, hid, gain, wr, meta, rows, wg, wu, wd,
               out, u_own, u_oth, gate_in, up_in, down_in, x_send, x_all, h_all, o_all, back,
               rows_oth, probs, local_sem, w_send, w_recv, d_send, d_recv, u_send, u_recv, x_ssem, x_rsem, b_send, b_recv):
    tok, d_model = hid.shape
    half = d_model // 2
    ff = wg.shape[2]
    fc = ff // FF_CHUNKS
    dc = half // HALF_CHUNKS
    n_dev = 8
    f = lax.axis_index('fsdp')
    j = lax.axis_index('ep')
    me = f * 4 + j
    j_low, j_high = lax.rem(j, 2), lax.div(j, 2)

    def peer(r):
        pf = 1 - f if r // 4 else f
        pj = (1 - j_low if r & 1 else j_low) + 2 * (1 - j_high if r & 2 else j_high)
        return pf, pj

    def remote(src, dst, ssem, rsem, r):
        pf, pj = peer(r)
        return pltpu.make_async_remote_copy(src_ref=src, dst_ref=dst, send_sem=ssem, recv_sem=rsem,
                                            device_id={'fsdp': pf, 'ep': pj}, device_id_type=MESH)

    def gate_copy(c):
        return remote(wg.at[1 - f, :, pl.ds(c * fc, fc)], gate_in.at[c], w_send.at[0, c], w_recv.at[0, c], 4)

    def up_copy(c):
        return remote(wu.at[1 - f, :, pl.ds(c * fc, fc)], up_in.at[c], w_send.at[1, c], w_recv.at[1, c], 4)

    def down_copy(q):
        return remote(wd.at[1 - f, :, pl.ds(q * dc, dc)], down_in.at[q], d_send.at[q], d_recv.at[q], 4)

    def rows_copy():
        return remote(rows, rows_oth, u_send.at[0], u_recv.at[0], 4)

    def u_copy():
        return remote(u_own, u_oth, u_send.at[1], u_recv.at[1], 4)

    def x_copy(s, r):
        pf, pj = peer(r)
        owner = me if s == 0 else (1 - f) * 4 + j
        return remote(x_send.at[s, pj], x_all.at[pl.ds(owner * cap, cap)], x_ssem.at[s, r], x_rsem.at[s, r], r)

    def back_copy(chunk, r):
        pf, pj = peer(r)
        return remote(o_all.at[chunk, pl.ds((pf * 4 + pj) * cap, cap)], back.at[chunk, pl.ds(me * cap, cap)],
                      b_send.at[chunk, r], b_recv.at[chunk, r], r)

    barrier = pltpu.get_barrier_semaphore()
    for r in range(1, n_dev):
        pf, pj = peer(r)
        pl.semaphore_signal(barrier, inc=1, device_id={'fsdp': pf, 'ep': pj}, device_id_type=MESH)
    pl.semaphore_wait(barrier, n_dev - 1)

    rows_copy().start()
    gate_copy(0).start()
    up_copy(0).start()

    def dispatch(u_buf, x_buf, onehot):
        block = 128
        load = pltpu.make_async_copy(hid, x_buf.at[pl.ds(0, tok)], local_sem.at[0])
        load.start()
        load.wait()
        gain_row = gain[...].astype(F32)
        lane = lax.broadcasted_iota(jnp.int32, (block, 128), 1)

        @pl.loop(0, tok // block)
        def _(i):
            here = pl.ds(pl.multiple_of(i * block, block), block)
            x = x_buf[here, :].astype(F32)
            mean_sq = jnp.mean(x * x, axis=-1, keepdims=True)
            u = (x * lax.rsqrt(mean_sq + EPS) * gain_row).astype(BF16)
            u_buf[here, :] = u
            logits = jnp.dot(u, wr[...], preferred_element_type=F32)
            info = meta[here, :]
            l0 = jnp.sum(jnp.where(lane == info[:, 0:1], logits, 0.0), axis=1, keepdims=True)
            l1 = jnp.sum(jnp.where(lane == info[:, 1:2], logits, 0.0), axis=1, keepdims=True)
            top = jnp.maximum(l0, l1)
            e0, e1 = jnp.exp(l0 - top), jnp.exp(l1 - top)
            total = e0 + e1
            probs[here, :] = jnp.where(lane == 0, e0 / total, e1 / total)

        keep = pltpu.make_async_copy(u_buf, u_own, local_sem.at[0])
        keep.start()
        keep.wait()
        u_copy().start()
        for c in range(1, FF_CHUNKS):
            gate_copy(c).start()
            up_copy(c).start()
        for q in range(HALF_CHUNKS):
            down_copy(q).start()

        for s in range(2):
            row_ref = rows if s == 0 else rows_oth
            owner = me if s == 0 else (1 - f) * 4 + j
            if s == 1:
                rows_copy().wait_recv()
                u_copy().wait_recv()
                load = pltpu.make_async_copy(u_oth, u_buf, local_sem.at[0])
                load.start()
                load.wait()

            @pl.loop(0, 4)
            def _(p):
                row = row_ref[pl.ds(f * 4 + p, 1), :]
                slot = lax.broadcasted_iota(jnp.int32, (cap, tok), 0)
                onehot[...] = jnp.where(slot == row, 1.0, 0.0).astype(BF16)

                @pl.loop(0, d_model // 256)
                def _(n):
                    cols = pl.ds(pl.multiple_of(n * 256, 256), 256)
                    x_buf[pl.ds(pl.multiple_of(p * cap, cap), cap), cols] = jnp.dot(
                        onehot[...], u_buf[:, cols], preferred_element_type=F32).astype(BF16)

                done = x_buf.at[pl.ds(pl.multiple_of(p * cap, cap), cap)]

                @pl.when(p == j)
                def _():
                    pltpu.make_async_copy(done, x_all.at[pl.ds(owner * cap, cap)], local_sem.at[p]).start()

                @pl.when(p != j)
                def _():
                    pltpu.make_async_copy(done, x_send.at[s, p], local_sem.at[p]).start()

            for p in range(4):
                pltpu.make_async_copy(x_buf.at[pl.ds(p * cap, cap)], x_send.at[s, p], local_sem.at[p]).wait()
            for r in (1, 2, 3):
                x_copy(s, r).start()

    pl.run_scoped(dispatch, pltpu.VMEM((tok, d_model), BF16), pltpu.VMEM((4 * cap, d_model), BF16), pltpu.VMEM((cap, tok), BF16))

    for s in range(2):
        for r in (1, 2, 3):
            x_copy(s, r).wait_recv()

    bm = 512
    sub = 256
    n_rows = n_dev * cap

    @pl.loop(0, FF_CHUNKS)
    def _(c):
        gate_copy(c).wait_recv()
        up_copy(c).wait_recv()

        def body(x_own, x_oth, g_own, g_oth, p_own, p_oth, h_ref):
            @pl.loop(0, bm // sub)
            def _(i):
                here = pl.ds(pl.multiple_of(i * sub, sub), sub)
                lhs_own, lhs_oth = x_own[here, :], x_oth[here, :]
                a = jnp.dot(lhs_own, g_own[...], preferred_element_type=F32) + jnp.dot(lhs_oth, g_oth[...], preferred_element_type=F32)
                b = jnp.dot(lhs_own, p_own[...], preferred_element_type=F32) + jnp.dot(lhs_oth, p_oth[...], preferred_element_type=F32)
                h_ref[here, :] = (a * jax.nn.sigmoid(a) * b).astype(BF16)

        pltpu.emit_pipeline(
            body, grid=(n_rows // bm,),
            in_specs=[pl.BlockSpec((bm, half), lambda i: (i, f)), pl.BlockSpec((bm, half), lambda i: (i, 1 - f)),
                      pl.BlockSpec((half, fc), lambda i: (0, c)), pl.BlockSpec((half, fc), lambda i: (0, 0)),
                      pl.BlockSpec((half, fc), lambda i: (0, c)), pl.BlockSpec((half, fc), lambda i: (0, 0))],
            out_specs=[pl.BlockSpec((bm, fc), lambda i: (i, c))],
        )(x_all, x_all, wg.at[f], gate_in.at[c], wu.at[f], up_in.at[c], h_all)

    def project(h_ref, w_ref, o_ref):
        @pl.loop(0, bm // sub)
        def _(i):
            here = pl.ds(pl.multiple_of(i * sub, sub), sub)
            o_ref[here, :] = jnp.dot(h_ref[here, :], w_ref[...], preferred_element_type=F32).astype(BF16)

    for phase in range(2):
        @pl.loop(0, HALF_CHUNKS)
        def _(q):
            if phase == 0:
                weight, col, chunk = wd.at[f], q, f * HALF_CHUNKS + q
            else:
                down_copy(q).wait_recv()
                weight, col, chunk = down_in.at[q], 0, (1 - f) * HALF_CHUNKS + q
            pltpu.emit_pipeline(
                project, grid=(n_rows // bm,),
                in_specs=[pl.BlockSpec((bm, ff), lambda i: (i, 0)), pl.BlockSpec((ff, dc), lambda i: (0, col))],
                out_specs=[pl.BlockSpec((bm, dc), lambda i: (i, 0))],
            )(h_all, weight, o_all.at[chunk])
            for r in range(1, n_dev):
                back_copy(chunk, r).start()

    def combine(b_buf, h_buf, onehot):
        block = 256

        @pl.loop(0, HALF_CHUNKS)
        def _(q):
            for side in range(2):
                chunk = side * HALF_CHUNKS + q
                cols = pl.ds(pl.multiple_of(chunk * dc, 128), dc)
                pltpu.make_async_copy(hid.at[:, cols], h_buf.at[side], local_sem.at[side]).start()
                for r in range(1, n_dev):
                    back_copy(chunk, r).wait_recv()
                for r in range(n_dev):
                    pf, pj = peer(r)
                    seg = pl.ds((pf * 4 + pj) * cap, cap)
                    src = back if r else o_all
                    pltpu.make_async_copy(src.at[chunk, seg], b_buf.at[seg, pl.ds(side * dc, dc)], local_sem.at[2 + side * 8 + r]).start()
            for side in range(2):
                chunk = side * HALF_CHUNKS + q
                cols = pl.ds(pl.multiple_of(chunk * dc, 128), dc)
                pltpu.make_async_copy(hid.at[:, cols], h_buf.at[side], local_sem.at[side]).wait()
                for r in range(n_dev):
                    pf, pj = peer(r)
                    seg = pl.ds((pf * 4 + pj) * cap, cap)
                    src = back if r else o_all
                    pltpu.make_async_copy(src.at[chunk, seg], b_buf.at[seg, pl.ds(side * dc, dc)], local_sem.at[2 + side * 8 + r]).wait()

            @pl.loop(0, tok // block)
            def _(i):
                here = pl.ds(pl.multiple_of(i * block, block), block)
                slot = lax.broadcasted_iota(jnp.int32, (block, n_rows), 1)
                info = meta[here, :]
                onehot[0:block, :] = jnp.where(slot == info[:, 2:3], 1.0, 0.0).astype(BF16)
                onehot[block:2 * block, :] = jnp.where(slot == info[:, 3:4], 1.0, 0.0).astype(BF16)
                p = probs[here, :]
                p0, p1 = p[:, 0:1], p[:, 1:2]
                picked = jnp.dot(onehot[...], b_buf[...], preferred_element_type=F32)
                for side in range(2):
                    part = picked[:, side * dc:(side + 1) * dc]
                    h_buf[side, here, :] = (h_buf[side, here, :].astype(F32) + (p0 * part[:block] + p1 * part[block:])).astype(BF16)

            for side in range(2):
                cols = pl.ds(pl.multiple_of((side * HALF_CHUNKS + q) * dc, 128), dc)
                pltpu.make_async_copy(h_buf.at[side], out.at[:, cols], local_sem.at[side]).start()
            for side in range(2):
                cols = pl.ds(pl.multiple_of((side * HALF_CHUNKS + q) * dc, 128), dc)
                pltpu.make_async_copy(h_buf.at[side], out.at[:, cols], local_sem.at[side]).wait()

    pl.run_scoped(combine, pltpu.VMEM((n_rows, 2 * dc), BF16), pltpu.VMEM((2, tok, dc), BF16), pltpu.VMEM((512, n_rows), BF16))

    rows_copy().wait_send()
    u_copy().wait_send()
    for c in range(FF_CHUNKS):
        gate_copy(c).wait_send()
        up_copy(c).wait_send()
    for q in range(HALF_CHUNKS):
        down_copy(q).wait_send()
    for s in range(2):
        for r in (1, 2, 3):
            x_copy(s, r).wait_send()

    @pl.loop(0, 2 * HALF_CHUNKS)
    def _(chunk):
        for r in range(1, n_dev):
            back_copy(chunk, r).wait_send()


def local_block(hidden, norm_gain, w_router, w_gate, w_up, w_down, top2_ids):
    tok, d_model = hidden.shape
    num_experts = w_router.shape[1]
    half, ff = w_gate.shape[1:]
    cap = (5 * tok + 2 * num_experts - 1) // (2 * num_experts)
    rows, slots = routes(top2_ids, num_experts, cap)
    meta = jnp.concatenate([top2_ids, slots], axis=1)
    router = jnp.pad(w_router, ((0, 0), (0, 128 - num_experts)))
    fc, dc = ff // FF_CHUNKS, half // HALF_CHUNKS
    n_rows = num_experts * cap
    shape = lambda *s: jax.ShapeDtypeStruct(s, BF16)
    dma = pltpu.SemaphoreType.DMA
    results = pl.pallas_call(
        functools.partial(moe_kernel, cap),
        out_shape=[shape(tok, d_model), shape(tok, d_model), shape(tok, d_model),
                   shape(FF_CHUNKS, half, fc), shape(FF_CHUNKS, half, fc), shape(HALF_CHUNKS, ff, dc),
                   shape(2, 4, cap, d_model), shape(n_rows, d_model), shape(n_rows, ff),
                   shape(2 * HALF_CHUNKS, n_rows, dc), shape(2 * HALF_CHUNKS, n_rows, dc)],
        in_specs=[ANY, VMEM, VMEM, VMEM, VMEM, ANY, ANY, ANY],
        out_specs=[ANY] * 11,
        scratch_shapes=[
            pltpu.VMEM((num_experts, tok), jnp.int32), pltpu.VMEM((tok, 128), F32),
            dma((18,)), dma((2, FF_CHUNKS)), dma((2, FF_CHUNKS)), dma((HALF_CHUNKS,)), dma((HALF_CHUNKS,)),
            dma((2,)), dma((2,)), dma((2, 4)), dma((2, 4)),
            dma((2 * HALF_CHUNKS, 8)), dma((2 * HALF_CHUNKS, 8))],
        compiler_params=pltpu.CompilerParams(collective_id=0, has_side_effects=True, vmem_limit_bytes=62 * 1024 * 1024),
    )(hidden, norm_gain[None, :], router, meta, rows, w_gate, w_up, w_down)
    return results[0]


def solution(mesh):
    tok_spec = P(('dp', 'fsdp', 'ep'), None)
    in_specs = (tok_spec, P(None), P(None, None), P('ep', 'fsdp', None), P('ep', 'fsdp', None), P('ep', None, 'fsdp'), tok_spec)
    return jax.shard_map(local_block, mesh=mesh, in_specs=in_specs, out_specs=tok_spec, check_vma=False)
```

time: 2630 us -> 1410 us (0.54)
  waiting for transfers between devices: 1580 us -> 0 us
  Pallas kernels: 0 us -> 1400 us
  matrix products: 497 us -> 1.42 us
  local copies, waits for them, and re-layouts: 266 us -> 12.7 us
  other arithmetic: 244 us -> 2.23 us
    pallas_call x0 -> x1, Pallas kernels: none -> 1400 us  [local_block(): pl.pallas_call(functools.partial(moe_kernel, cap), out_shape=[shape(tok,...]
    all_gather x3 -> x0, waiting for transfers between devices: 1100 us -> none  [the longest x1 453 us: local_block(): gate_full = lax.all_gather(w_gate, 'fsdp', axis=1, tiled=True)]
    dot_general x4 -> x1, matrix products: 497 us -> 1.42 us  [routes(): jnp.dot(before, chosen.astype(BF16), preferred_element_type=F32)]
    all_to_all x2 -> x0, waiting for transfers between devices: 472 us -> none  [the longest x1 254 us: local_block(): recv_rows = lax.all_to_all(send_rows, 'ep', 0, 1, tiled=True)]
    reduce_sum x4 -> x1, other arithmetic: 201 us -> 0.05 us  [routes(): slots = jnp.sum(jnp.where(choice, flat[:, None, :], 0), axis=2)]
    gather x8 -> x0, local copies, waits for them, and re-layouts: 158 us -> none  [the longest x2 82.5 us: take_slots(): return jnp.take(expert_rows, slot_ids, axis=0, mode='fill', fill_value=0)]
    convert_element_type x1 -> x0, local copies, waits for them, and re-layouts: 43 us -> none  [expert_block(): jnp.einsum('ecf,efd->ecd', hidden_act, down_full, preferred_element_type=...]
    all_to_all x2 -> x0, local copies, waits for them, and re-layouts: 42.3 us -> none  [the longest x1 22.5 us: local_block(): back_rows = lax.all_to_all(expert_out, 'ep', 1, 0, tiled=True)]
  transfers between devices with their start and end apart: 5 -> 0, of which waited for: 5 -> 0; matrix products, arithmetic and copies ran while one was open for 19% -> 0% of each run, Pallas kernels for 0% -> 0%
where the time goes in v1:
time: 1410 us
  Pallas kernels  1400 us (99%)
    pallas_call x1, Pallas kernels, local_block(): pl.pallas_call(functools.partial(moe_kernel, cap), out_shape=[shape(tok,...  1400 us

profile of v1, /device:TPU:1, one launch (start us, length us, event | category | flops | bytes accessed | tf_op | source)
XLA Modules:
  0.0 1412.7 jit_solution(2237603148016435066)
XLA Ops:
  0.0 1.3 broadcast_in_dim.28.gain
  1.3 0.8 fusion.5
  2.1 1.4 add_select_fusion
  3.5 0.1 select_reduce_fusion
  3.6 0.7 pad_add_fusion
  4.3 0.6 bitcast_select_fusion.rows
  5.0 1.1 copy.16
  6.1 0.9 pad.4.wr
  7.0 1.3 copy.17.meta
  8.3 1396.3 %shard_map.73 = (bf16[2048,2304]{1,0:T(8,128)(2,1)}, bf16[2048,2304]{1,0:T(8,128)(2,1)}, bf16[2048,2304]{1,0:T(8,128)(2,1)}, bf16[5,1152,1152]{2,1,0:T(8,128)(2,...) custom-call(bf16[2048,2304]{1,0:T(8,128)(2,1)} %hid.1, ...), custom_call_target="tpu_custom_call" | custom-call | tf_op jit(solution)/shard_map/pallas_call | solution.py:297
  1404.7 8.0 copy.19
  (2 shorter events, 0.0 us)

commit v2 on v1

--- a/solution.py
+++ b/solution.py
@@ -15,32 +15,22 @@
 BF16 = jnp.bfloat16
 FF_CHUNKS = 5
 HALF_CHUNKS = 3
-
-
-def routes(top2_ids, num_experts, capacity):
-    tok = top2_ids.shape[0]
-    place = (top2_ids % 2) * (num_experts // 2) + top2_ids // 2
-    choice = place[:, :, None] == jnp.arange(num_experts, dtype=jnp.int32)
-    chosen = jnp.any(choice, axis=1)
-    step = jnp.arange(tok, dtype=jnp.int32)
-    before = (step[:, None] > step[None, :]).astype(BF16)
-    position = jnp.dot(before, chosen.astype(BF16), preferred_element_type=F32).astype(jnp.int32)
-    kept = jnp.where(chosen & (position < capacity), position, -1)
-    base = jnp.arange(num_experts, dtype=jnp.int32) * capacity
-    flat = jnp.where(kept >= 0, kept + base, -1)
-    slots = jnp.sum(jnp.where(choice, flat[:, None, :], 0), axis=2)
-    return kept.T, slots
-
-
-def moe_kernel(cap, hid, gain, wr, meta, rows, wg, wu, wd,
+PIECE = 128
+TOK = 128
+WINDOW = TOK + 16
+
+
+def moe_kernel(cap, hid, gain, wr, ids, wg, wu, wd,
                out, u_own, u_oth, gate_in, up_in, down_in, x_send, x_all, h_all, o_all, back,
-               rows_oth, probs, local_sem, w_send, w_recv, d_send, d_recv, u_send, u_recv, x_ssem, x_rsem, b_send, b_recv):
+               rows, rows_oth, meta, probs, wr_pad, base_v, base_s, local_sem, w_send, w_recv, d_send, d_recv, u_send, u_recv, x_ssem, x_rsem, b_send, b_recv):
     tok, d_model = hid.shape
     half = d_model // 2
     ff = wg.shape[2]
     fc = ff // FF_CHUNKS
     dc = half // HALF_CHUNKS
     n_dev = 8
+    pieces = dc // PIECE
+    n_rows = n_dev * cap
     f = lax.axis_index('fsdp')
     j = lax.axis_index('ep')
     me = f * 4 + j
@@ -76,10 +66,11 @@
         owner = me if s == 0 else (1 - f) * 4 + j
         return remote(x_send.at[s, pj], x_all.at[pl.ds(owner * cap, cap)], x_ssem.at[s, r], x_rsem.at[s, r], r)
 
-    def back_copy(chunk, r):
+    def back_copy(chunk, k, r):
         pf, pj = peer(r)
-        return remote(o_all.at[chunk, pl.ds((pf * 4 + pj) * cap, cap)], back.at[chunk, pl.ds(me * cap, cap)],
-                      b_send.at[chunk, r], b_recv.at[chunk, r], r)
+        cols = pl.ds(pl.multiple_of(k * PIECE, PIECE), PIECE)
+        return remote(o_all.at[chunk, pl.ds((pf * 4 + pj) * cap, cap), cols], back.at[chunk, pl.ds(me * cap, cap), cols],
+                      b_send.at[chunk * pieces + k, r], b_recv.at[chunk * pieces + k, r], r)
 
     barrier = pltpu.get_barrier_semaphore()
     for r in range(1, n_dev):
@@ -87,16 +78,47 @@
         pl.semaphore_signal(barrier, inc=1, device_id={'fsdp': pf, 'ep': pj}, device_id_type=MESH)
     pl.semaphore_wait(barrier, n_dev - 1)
 
-    rows_copy().start()
     gate_copy(0).start()
     up_copy(0).start()
+
+    wr_pad[...] = jnp.zeros_like(wr_pad)
+    wr_pad[0:n_dev, :] = wr[...]
+    tri = (lax.broadcasted_iota(jnp.int32, (TOK, TOK), 0) < lax.broadcasted_iota(jnp.int32, (TOK, TOK), 1)).astype(F32).astype(BF16)
+    spot = lax.broadcasted_iota(jnp.int32, (n_dev, TOK), 0)
+    column = lax.broadcasted_iota(jnp.int32, (n_dev, TOK), 1)
+    line = lax.broadcasted_iota(jnp.int32, (TOK, TOK), 0)
+
+    def route(blk, carry):
+        count, bases = carry
+        here = pl.ds(pl.multiple_of(blk * TOK, TOK), TOK)
+        id0, id1 = ids[0:1, here], ids[1:2, here]
+        place0 = lax.rem(id0, 2) * 4 + lax.div(id0, 2)
+        place1 = lax.rem(id1, 2) * 4 + lax.div(id1, 2)
+        chosen = (spot == place0) | (spot == place1)
+        before = jnp.dot(jnp.where(chosen, 1.0, 0.0).astype(BF16), tri, preferred_element_type=F32)
+        position = before.astype(jnp.int32) + count
+        kept = jnp.where(chosen & (position < cap), position, -1)
+        rows[:, here] = kept
+        flat = jnp.where(kept >= 0, kept + spot * cap, -1)
+        slot0 = jnp.sum(jnp.where(spot == place0, flat, 0), axis=0, keepdims=True)
+        slot1 = jnp.sum(jnp.where(spot == place1, flat, 0), axis=0, keepdims=True)
+        stacked = jnp.where(line == 0, id0, jnp.where(line == 1, id1, jnp.where(line == 2, slot0, slot1)))
+        meta[here, :] = stacked.astype(F32).T.astype(jnp.int32)
+        start = jnp.minimum(lax.div(count, 16), (cap - WINDOW) // 16)
+        bases = jnp.where(column == blk, start + spot * (cap // 16), bases)
+        return count + jnp.sum(jnp.where(chosen, 1, 0), axis=1, keepdims=True), bases
+
+    bases = lax.fori_loop(0, tok // TOK, route, (jnp.zeros((n_dev, 1), jnp.int32), jnp.zeros((n_dev, TOK), jnp.int32)))[1]
+    base_v[...] = bases
 
     def dispatch(u_buf, x_buf, onehot):
         block = 128
         load = pltpu.make_async_copy(hid, x_buf.at[pl.ds(0, tok)], local_sem.at[0])
         load.start()
+        pltpu.make_async_copy(base_v, base_s, local_sem.at[1]).start()
         load.wait()
-        gain_row = gain[...].astype(F32)
+        pltpu.make_async_copy(base_v, base_s, local_sem.at[1]).wait()
+        gain_row = gain[...].astype(F32)[None, :]
         lane = lax.broadcasted_iota(jnp.int32, (block, 128), 1)
 
         @pl.loop(0, tok // block)
@@ -106,7 +128,7 @@
             mean_sq = jnp.mean(x * x, axis=-1, keepdims=True)
             u = (x * lax.rsqrt(mean_sq + EPS) * gain_row).astype(BF16)
             u_buf[here, :] = u
-            logits = jnp.dot(u, wr[...], preferred_element_type=F32)
+            logits = lax.dot_general(u, wr_pad[...], (((1,), (1,)), ((), ())), preferred_element_type=F32)
             info = meta[here, :]
             l0 = jnp.sum(jnp.where(lane == info[:, 0:1], logits, 0.0), axis=1, keepdims=True)
             l1 = jnp.sum(jnp.where(lane == info[:, 1:2], logits, 0.0), axis=1, keepdims=True)
@@ -118,6 +140,7 @@
         keep = pltpu.make_async_copy(u_buf, u_own, local_sem.at[0])
         keep.start()
         keep.wait()
+        rows_copy().start()
         u_copy().start()
         for c in range(1, FF_CHUNKS):
             gate_copy(c).start()
@@ -170,7 +193,6 @@
 
     bm = 512
     sub = 256
-    n_rows = n_dev * cap
 
     @pl.loop(0, FF_CHUNKS)
     def _(c):
@@ -213,57 +235,72 @@
                 in_specs=[pl.BlockSpec((bm, ff), lambda i: (i, 0)), pl.BlockSpec((ff, dc), lambda i: (0, col))],
                 out_specs=[pl.BlockSpec((bm, dc), lambda i: (i, 0))],
             )(h_all, weight, o_all.at[chunk])
-            for r in range(1, n_dev):
-                back_copy(chunk, r).start()
-
-    def combine(b_buf, h_buf, onehot):
-        block = 256
-
-        @pl.loop(0, HALF_CHUNKS)
-        def _(q):
-            for side in range(2):
-                chunk = side * HALF_CHUNKS + q
-                cols = pl.ds(pl.multiple_of(chunk * dc, 128), dc)
-                pltpu.make_async_copy(hid.at[:, cols], h_buf.at[side], local_sem.at[side]).start()
+            for k in range(pieces):
                 for r in range(1, n_dev):
-                    back_copy(chunk, r).wait_recv()
+                    back_copy(chunk, k, r).start()
+
+    def combine(b_buf, h_buf, picks, window):
+        n_blocks = tok // TOK
+        lane = lax.broadcasted_iota(jnp.int32, (1, n_dev * WINDOW), 1)
+
+        @pl.loop(0, n_blocks)
+        def _(i):
+            shift = jnp.zeros_like(lane)
+            for e in range(n_dev):
+                shift = jnp.where(lane >= e * WINDOW, base_s[e, i] * 16 - e * WINDOW, shift)
+            row = lane + shift
+            info = meta[pl.ds(pl.multiple_of(i * TOK, TOK), TOK), :]
+            for k in range(2):
+                picks[i, k * TOK:(k + 1) * TOK, :] = jnp.where(row == info[:, 2 + k:3 + k], 1.0, 0.0).astype(BF16)
+
+        @pl.loop(0, HALF_CHUNKS * pieces)
+        def _(step):
+            q, k = lax.div(step, pieces), lax.rem(step, pieces)
+            piece = pl.ds(pl.multiple_of(k * PIECE, PIECE), PIECE)
+
+            def cols(side):
+                return pl.ds(pl.multiple_of((side * HALF_CHUNKS + q) * dc + k * PIECE, PIECE), PIECE)
+
+            def loads(side):
+                moves = [pltpu.make_async_copy(hid.at[:, cols(side)], h_buf.at[side], local_sem.at[side])]
                 for r in range(n_dev):
                     pf, pj = peer(r)
                     seg = pl.ds((pf * 4 + pj) * cap, cap)
                     src = back if r else o_all
-                    pltpu.make_async_copy(src.at[chunk, seg], b_buf.at[seg, pl.ds(side * dc, dc)], local_sem.at[2 + side * 8 + r]).start()
+                    moves.append(pltpu.make_async_copy(src.at[side * HALF_CHUNKS + q, seg, piece], b_buf.at[seg, pl.ds(side * PIECE, PIECE)], local_sem.at[2 + side * 8 + r]))
+                return moves
+
+            def store(side):
+                return pltpu.make_async_copy(h_buf.at[side], out.at[:, cols(side)], local_sem.at[side])
+
             for side in range(2):
-                chunk = side * HALF_CHUNKS + q
-                cols = pl.ds(pl.multiple_of(chunk * dc, 128), dc)
-                pltpu.make_async_copy(hid.at[:, cols], h_buf.at[side], local_sem.at[side]).wait()
-                for r in range(n_dev):
-                    pf, pj = peer(r)
-                    seg = pl.ds((pf * 4 + pj) * cap, cap)
-                    src = back if r else o_all
-                    pltpu.make_async_copy(src.at[chunk, seg], b_buf.at[seg, pl.ds(side * dc, dc)], local_sem.at[2 + side * 8 + r]).wait()
-
-            @pl.loop(0, tok // block)
+                for r in range(1, n_dev):
+                    back_copy(side * HALF_CHUNKS + q, k, r).wait_recv()
+                for move in loads(side):
+                    move.start()
+            for side in range(2):
+                for move in loads(side):
+                    move.wait()
+
+            @pl.loop(0, n_blocks)
             def _(i):
-                here = pl.ds(pl.multiple_of(i * block, block), block)
-                slot = lax.broadcasted_iota(jnp.int32, (block, n_rows), 1)
-                info = meta[here, :]
-                onehot[0:block, :] = jnp.where(slot == info[:, 2:3], 1.0, 0.0).astype(BF16)
-                onehot[block:2 * block, :] = jnp.where(slot == info[:, 3:4], 1.0, 0.0).astype(BF16)
+                here = pl.ds(pl.multiple_of(i * TOK, TOK), TOK)
+                for e in range(n_dev):
+                    window[e * WINDOW:(e + 1) * WINDOW, :] = b_buf[pl.ds(base_s[e, i] * 16, WINDOW), :]
                 p = probs[here, :]
                 p0, p1 = p[:, 0:1], p[:, 1:2]
-                picked = jnp.dot(onehot[...], b_buf[...], preferred_element_type=F32)
+                picked = jnp.dot(picks[i], window[...], preferred_element_type=F32)
+                moe = p0 * picked[:TOK] + p1 * picked[TOK:]
                 for side in range(2):
-                    part = picked[:, side * dc:(side + 1) * dc]
-                    h_buf[side, here, :] = (h_buf[side, here, :].astype(F32) + (p0 * part[:block] + p1 * part[block:])).astype(BF16)
+                    h_buf[side, here, :] = (h_buf[side, here, :].astype(F32) + moe[:, side * PIECE:(side + 1) * PIECE]).astype(BF16)
 
             for side in range(2):
-                cols = pl.ds(pl.multiple_of((side * HALF_CHUNKS + q) * dc, 128), dc)
-                pltpu.make_async_copy(h_buf.at[side], out.at[:, cols], local_sem.at[side]).start()
+                store(side).start()
             for side in range(2):
-                cols = pl.ds(pl.multiple_of((side * HALF_CHUNKS + q) * dc, 128), dc)
-                pltpu.make_async_copy(h_buf.at[side], out.at[:, cols], local_sem.at[side]).wait()
-
-    pl.run_scoped(combine, pltpu.VMEM((n_rows, 2 * dc), BF16), pltpu.VMEM((2, tok, dc), BF16), pltpu.VMEM((512, n_rows), BF16))
+                store(side).wait()
+
+    pl.run_scoped(combine, pltpu.VMEM((n_rows, 2 * PIECE), BF16), pltpu.VMEM((2, tok, PIECE), BF16),
+                  pltpu.VMEM((tok // TOK, 2 * TOK, n_dev * WINDOW), BF16), pltpu.VMEM((n_dev * WINDOW, 2 * PIECE), BF16))
 
     rows_copy().wait_send()
     u_copy().wait_send()
@@ -278,8 +315,9 @@
 
     @pl.loop(0, 2 * HALF_CHUNKS)
     def _(chunk):
-        for r in range(1, n_dev):
-            back_copy(chunk, r).wait_send()
+        for k in range(pieces):
+            for r in range(1, n_dev):
+                back_copy(chunk, k, r).wait_send()
 
 
 def local_block(hidden, norm_gain, w_router, w_gate, w_up, w_down, top2_ids):
@@ -287,9 +325,6 @@
     num_experts = w_router.shape[1]
     half, ff = w_gate.shape[1:]
     cap = (5 * tok + 2 * num_experts - 1) // (2 * num_experts)
-    rows, slots = routes(top2_ids, num_experts, cap)
-    meta = jnp.concatenate([top2_ids, slots], axis=1)
-    router = jnp.pad(w_router, ((0, 0), (0, 128 - num_experts)))
     fc, dc = ff // FF_CHUNKS, half // HALF_CHUNKS
     n_rows = num_experts * cap
     shape = lambda *s: jax.ShapeDtypeStruct(s, BF16)
@@ -300,15 +335,17 @@
                    shape(FF_CHUNKS, half, fc), shape(FF_CHUNKS, half, fc), shape(HALF_CHUNKS, ff, dc),
                    shape(2, 4, cap, d_model), shape(n_rows, d_model), shape(n_rows, ff),
                    shape(2 * HALF_CHUNKS, n_rows, dc), shape(2 * HALF_CHUNKS, n_rows, dc)],
-        in_specs=[ANY, VMEM, VMEM, VMEM, VMEM, ANY, ANY, ANY],
+        in_specs=[ANY, VMEM, VMEM, VMEM, ANY, ANY, ANY],
         out_specs=[ANY] * 11,
         scratch_shapes=[
-            pltpu.VMEM((num_experts, tok), jnp.int32), pltpu.VMEM((tok, 128), F32),
+            pltpu.VMEM((num_experts, tok), jnp.int32), pltpu.VMEM((num_experts, tok), jnp.int32),
+            pltpu.VMEM((tok, 128), jnp.int32), pltpu.VMEM((tok, 128), F32), pltpu.VMEM((128, d_model), BF16),
+            pltpu.VMEM((num_experts, TOK), jnp.int32), pltpu.SMEM((num_experts, TOK), jnp.int32),
             dma((18,)), dma((2, FF_CHUNKS)), dma((2, FF_CHUNKS)), dma((HALF_CHUNKS,)), dma((HALF_CHUNKS,)),
             dma((2,)), dma((2,)), dma((2, 4)), dma((2, 4)),
-            dma((2 * HALF_CHUNKS, 8)), dma((2 * HALF_CHUNKS, 8))],
+            dma((d_model // PIECE, 8)), dma((d_model // PIECE, 8))],
         compiler_params=pltpu.CompilerParams(collective_id=0, has_side_effects=True, vmem_limit_bytes=62 * 1024 * 1024),
-    )(hidden, norm_gain[None, :], router, meta, rows, w_gate, w_up, w_down)
+    )(hidden, norm_gain, w_router.T, top2_ids.T, w_gate, w_up, w_down)
     return results[0]
 
 

time: 1410 us -> 1350 us (0.957)
  Pallas kernels: 1400 us -> 1340 us
    pallas_call x1, Pallas kernels: 1400 us -> 1340 us  [local_block(): pl.pallas_call(functools.partial(moe_kernel, cap), out_shape=[shape(tok,...]
where the time goes in v2:
time: 1350 us
  Pallas kernels  1340 us (99%)
    pallas_call x1, Pallas kernels, local_block(): pl.pallas_call(functools.partial(moe_kernel, cap), out_shape=[shape(tok,...  1340 us

profile of v2, /device:TPU:1, one launch (start us, length us, event | category | flops | bytes accessed | tf_op | source)
XLA Modules:
  0.0 1350.0 jit_solution(8062518434322375495)
XLA Ops:
  0.0 1341.9 %shard_map.73 = (bf16[2048,2304]{1,0:T(8,128)(2,1)}, bf16[2048,2304]{1,0:T(8,128)(2,1)}, bf16[2048,2304]{1,0:T(8,128)(2,1)}, bf16[5,1152,1152]{2,1,0:T(8,128)(2,...) custom-call(bf16[2048,2304]{1,0:T(8,128)(2,1)} %hid.1, ...), custom_call_target="tpu_custom_call" | custom-call | tf_op jit(solution)/shard_map/pallas_call | solution.py:332
  1341.9 8.0 copy.9

commit v3 on v2

v3 whole, which is shorter than its diff:
```python
import functools

import jax
import jax.numpy as jnp
from jax import lax
from jax.experimental import pallas as pl
from jax.experimental.pallas import tpu as pltpu
from jax.sharding import PartitionSpec as P

EPS = 1e-5
MESH = pl.DeviceIdType.MESH
ANY = pl.BlockSpec(memory_space=pl.ANY)
VMEM = pl.BlockSpec(memory_space=pltpu.VMEM)
F32 = jnp.float32
BF16 = jnp.bfloat16
FF_CHUNKS = 5
HALF_CHUNKS = 3
PIECE = 128
TOK = 128
WINDOW = TOK + 16


def moe_kernel(cap, hid, gain, wr, ids, wg, wu, wd,
               out, hid_oth, gate_in, up_in, down_in, x_send, x_all, h_all, o_all, back, y_own, y_oth,
               rows, ids_oth, meta, probs, wr_pad, base_v, base_s, local_sem, w_send, w_recv, d_send, d_recv,
               u_send, u_recv, x_ssem, x_rsem, b_send, b_recv, y_send, y_recv):
    tok, d_model = hid.shape
    half = d_model // 2
    ff = wg.shape[2]
    fc = ff // FF_CHUNKS
    dc = half // HALF_CHUNKS
    n_dev = 8
    pieces = dc // PIECE
    n_rows = n_dev * cap
    chunks = 2 * HALF_CHUNKS
    n_blocks = tok // TOK
    f = lax.axis_index('fsdp')
    j = lax.axis_index('ep')
    me = f * 4 + j
    j_low, j_high = lax.rem(j, 2), lax.div(j, 2)

    def peer(r):
        pf = 1 - f if r // 4 else f
        pj = (1 - j_low if r & 1 else j_low) + 2 * (1 - j_high if r & 2 else j_high)
        return pf, pj

    def remote(src, dst, ssem, rsem, r):
        pf, pj = peer(r)
        return pltpu.make_async_remote_copy(src_ref=src, dst_ref=dst, send_sem=ssem, recv_sem=rsem,
                                            device_id={'fsdp': pf, 'ep': pj}, device_id_type=MESH)

    def gate_copy(c):
        return remote(wg.at[1 - f, :, pl.ds(c * fc, fc)], gate_in.at[c], w_send.at[0, c], w_recv.at[0, c], 4)

    def up_copy(c):
        return remote(wu.at[1 - f, :, pl.ds(c * fc, fc)], up_in.at[c], w_send.at[1, c], w_recv.at[1, c], 4)

    def down_copy(q):
        return remote(wd.at[1 - f, :, pl.ds(q * dc, dc)], down_in.at[q], d_send.at[q], d_recv.at[q], 4)

    def ids_copy():
        return remote(ids, ids_oth, u_send.at[0], u_recv.at[0], 4)

    def hid_copy():
        return remote(hid, hid_oth, u_send.at[1], u_recv.at[1], 4)

    def x_copy(s, r):
        pf, pj = peer(r)
        owner = me if s == 0 else (1 - f) * 4 + j
        return remote(x_send.at[s, pj], x_all.at[pl.ds(owner * cap, cap)], x_ssem.at[s, r], x_rsem.at[s, r], r)

    def back_copy(s, chunk, r):
        pf, pj = peer(r)
        owner = (f if s == 0 else 1 - f) * 4 + pj
        return remote(o_all.at[chunk, pl.ds(owner * cap, cap)], back.at[s, chunk, pl.ds(j * cap, cap)],
                      b_send.at[s * chunks + chunk, r], b_recv.at[s * chunks + chunk, r], r)

    def y_copy(piece):
        return remote(y_own.at[piece], y_oth.at[piece], y_send.at[piece], y_recv.at[piece], 4)

    barrier = pltpu.get_barrier_semaphore()
    for r in range(1, n_dev):
        pf, pj = peer(r)
        pl.semaphore_signal(barrier, inc=1, device_id={'fsdp': pf, 'ep': pj}, device_id_type=MESH)
    pl.semaphore_wait(barrier, n_dev - 1)

    ids_copy().start()
    hid_copy().start()
    for c in range(FF_CHUNKS):
        gate_copy(c).start()
        up_copy(c).start()
    for q in range(HALF_CHUNKS):
        down_copy(q).start()

    wr_pad[...] = jnp.zeros_like(wr_pad)
    wr_pad[0:n_dev, :] = wr[...]
    tri = (lax.broadcasted_iota(jnp.int32, (TOK, TOK), 0) < lax.broadcasted_iota(jnp.int32, (TOK, TOK), 1)).astype(F32).astype(BF16)
    spot = lax.broadcasted_iota(jnp.int32, (n_dev, TOK), 0)
    column = lax.broadcasted_iota(jnp.int32, (n_dev, TOK), 1)
    line = lax.broadcasted_iota(jnp.int32, (TOK, TOK), 0)

    def route(s, ids_ref, blk, carry):
        count, bases = carry
        here = pl.ds(pl.multiple_of(blk * TOK, TOK), TOK)
        id0, id1 = ids_ref[0:1, here], ids_ref[1:2, here]
        place0 = lax.rem(id0, 2) * 4 + lax.div(id0, 2)
        place1 = lax.rem(id1, 2) * 4 + lax.div(id1, 2)
        chosen = (spot == place0) | (spot == place1)
        before = jnp.dot(jnp.where(chosen, 1.0, 0.0).astype(BF16), tri, preferred_element_type=F32)
        position = before.astype(jnp.int32) + count
        kept = jnp.where(chosen & (position < cap), position, -1)
        rows[:, here] = kept
        mine = (spot >= f * 4) & (spot < f * 4 + 4)
        flat = jnp.where(mine & (kept >= 0), kept + (spot - f * 4) * cap, -1)
        slot0 = jnp.sum(jnp.where(spot == place0, flat, 0), axis=0, keepdims=True)
        slot1 = jnp.sum(jnp.where(spot == place1, flat, 0), axis=0, keepdims=True)
        stacked = jnp.where(line == 0, id0, jnp.where(line == 1, id1, jnp.where(line == 2, slot0, slot1)))
        meta[s, here, :] = stacked.astype(F32).T.astype(jnp.int32)
        start = jnp.minimum(lax.div(count, 16), (cap - WINDOW) // 16)
        bases = jnp.where(column == blk, start + lax.rem(spot, 4) * (cap // 16), bases)
        return count + jnp.sum(jnp.where(chosen, 1, 0), axis=1, keepdims=True), bases

    def dispatch(u_buf, x_buf, onehot):
        block = 128
        gain_row = gain[...].astype(F32)[None, :]
        lane = lax.broadcasted_iota(jnp.int32, (block, 128), 1)

        for s in range(2):
            owner = me if s == 0 else (1 - f) * 4 + j
            if s == 1:
                ids_copy().wait_recv()
                hid_copy().wait_recv()
            load = pltpu.make_async_copy(hid if s == 0 else hid_oth, x_buf.at[pl.ds(0, tok)], local_sem.at[0])
            load.start()
            base_v[s] = lax.fori_loop(0, n_blocks, functools.partial(route, s, ids if s == 0 else ids_oth),
                                      (jnp.zeros((n_dev, 1), jnp.int32), jnp.zeros((n_dev, TOK), jnp.int32)))[1]
            load.wait()

            @pl.loop(0, tok // block)
            def _(i):
                here = pl.ds(pl.multiple_of(i * block, block), block)
                x = x_buf[here, :].astype(F32)
                mean_sq = jnp.mean(x * x, axis=-1, keepdims=True)
                u = (x * lax.rsqrt(mean_sq + EPS) * gain_row).astype(BF16)
                u_buf[here, :] = u
                logits = lax.dot_general(u, wr_pad[...], (((1,), (1,)), ((), ())), preferred_element_type=F32)
                info = meta[s, here, :]
                l0 = jnp.sum(jnp.where(lane == info[:, 0:1], logits, 0.0), axis=1, keepdims=True)
                l1 = jnp.sum(jnp.where(lane == info[:, 1:2], logits, 0.0), axis=1, keepdims=True)
                top = jnp.maximum(l0, l1)
                e0, e1 = jnp.exp(l0 - top), jnp.exp(l1 - top)
                total = e0 + e1
                probs[s, here, :] = jnp.where(lane == 0, e0 / total, e1 / total)

            @pl.loop(0, 4)
            def _(p):
                row = rows[pl.ds(f * 4 + p, 1), :]
                slot = lax.broadcasted_iota(jnp.int32, (cap, tok), 0)
                onehot[...] = jnp.where(slot == row, 1.0, 0.0).astype(BF16)

                @pl.loop(0, d_model // 256)
                def _(n):
                    cols = pl.ds(pl.multiple_of(n * 256, 256), 256)
                    x_buf[pl.ds(pl.multiple_of(p * cap, cap), cap), cols] = jnp.dot(
                        onehot[...], u_buf[:, cols], preferred_element_type=F32).astype(BF16)

                done = x_buf.at[pl.ds(pl.multiple_of(p * cap, cap), cap)]

                @pl.when(p == j)
                def _():
                    pltpu.make_async_copy(done, x_all.at[pl.ds(owner * cap, cap)], local_sem.at[p]).start()

                @pl.when(p != j)
                def _():
                    pltpu.make_async_copy(done, x_send.at[s, p], local_sem.at[p]).start()

            for p in range(4):
                pltpu.make_async_copy(x_buf.at[pl.ds(p * cap, cap)], x_send.at[s, p], local_sem.at[p]).wait()
            for r in (1, 2, 3):
                x_copy(s, r).start()

        move = pltpu.make_async_copy(base_v, base_s, local_sem.at[0])
        move.start()
        move.wait()

    pl.run_scoped(dispatch, pltpu.VMEM((tok, d_model), BF16), pltpu.VMEM((4 * cap, d_model), BF16), pltpu.VMEM((cap, tok), BF16))

    for s in range(2):
        for r in (1, 2, 3):
            x_copy(s, r).wait_recv()

    bm = 512
    sub = 256

    @pl.loop(0, FF_CHUNKS)
    def _(c):
        gate_copy(c).wait_recv()
        up_copy(c).wait_recv()

        def body(x_own, x_oth, g_own, g_oth, p_own, p_oth, h_ref):
            @pl.loop(0, bm // sub)
            def _(i):
                here = pl.ds(pl.multiple_of(i * sub, sub), sub)
                lhs_own, lhs_oth = x_own[here, :], x_oth[here, :]
                a = jnp.dot(lhs_own, g_own[...], preferred_element_type=F32) + jnp.dot(lhs_oth, g_oth[...], preferred_element_type=F32)
                b = jnp.dot(lhs_own, p_own[...], preferred_element_type=F32) + jnp.dot(lhs_oth, p_oth[...], preferred_element_type=F32)
                h_ref[here, :] = (a * jax.nn.sigmoid(a) * b).astype(BF16)

        pltpu.emit_pipeline(
            body, grid=(n_rows // bm,),
            in_specs=[pl.BlockSpec((bm, half), lambda i: (i, f)), pl.BlockSpec((bm, half), lambda i: (i, 1 - f)),
                      pl.BlockSpec((half, fc), lambda i: (0, c)), pl.BlockSpec((half, fc), lambda i: (0, 0)),
                      pl.BlockSpec((half, fc), lambda i: (0, c)), pl.BlockSpec((half, fc), lambda i: (0, 0))],
            out_specs=[pl.BlockSpec((bm, fc), lambda i: (i, c))],
        )(x_all, x_all, wg.at[f], gate_in.at[c], wu.at[f], up_in.at[c], h_all)

    def project(h_ref, w_ref, o_ref):
        @pl.loop(0, bm // sub)
        def _(i):
            here = pl.ds(pl.multiple_of(i * sub, sub), sub)
            o_ref[here, :] = jnp.dot(h_ref[here, :], w_ref[...], preferred_element_type=F32).astype(BF16)

    def finish(picks, segs, mix, seg_piece, mix_piece, y_piece, window, window_piece):
        side_rows = 4 * WINDOW
        lane = lax.broadcasted_iota(jnp.int32, (1, side_rows), 1)

        def expert_out(phase, q):
            if phase == 0:
                weight, col, chunk = wd.at[f], q, f * HALF_CHUNKS + q
            else:
                down_copy(q).wait_recv()
                weight, col, chunk = down_in.at[q], 0, (1 - f) * HALF_CHUNKS + q
            pltpu.emit_pipeline(
                project, grid=(n_rows // bm,),
                in_specs=[pl.BlockSpec((bm, ff), lambda i: (i, 0)), pl.BlockSpec((ff, dc), lambda i: (0, col))],
                out_specs=[pl.BlockSpec((bm, dc), lambda i: (i, 0))],
            )(h_all, weight, o_all.at[chunk])
            for s in (1, 0):
                for r in (1, 2, 3):
                    back_copy(s, chunk, r).start()

        def fill(s, chunk, cols, buf):
            moves = []
            for r in range(4):
                pj = peer(r)[1]
                owner = (f if s == 0 else 1 - f) * 4 + j
                src = back.at[s, chunk, pl.ds(pj * cap, cap), cols] if r else o_all.at[chunk, pl.ds(owner * cap, cap), cols]
                moves.append(pltpu.make_async_copy(src, buf.at[pl.ds(pj * cap, cap)], local_sem.at[2 + r]))
            return moves

        def take(s, i, buf, win):
            for p in range(4):
                win[p * WINDOW:(p + 1) * WINDOW, :] = buf[pl.ds(base_s[s, f * 4 + p, i] * 16, WINDOW), :]
            picked = jnp.dot(picks[s, i], win[...], preferred_element_type=F32)
            return picked[:TOK], picked[TOK:]

        def relay(half_id, q):
            chunk = half_id * HALF_CHUNKS + q
            for r in (1, 2, 3):
                back_copy(1, chunk, r).wait_recv()
            cols = pl.ds(pl.multiple_of(chunk * dc, PIECE), dc)
            moves = fill(1, chunk, pl.ds(0, dc), segs) + [pltpu.make_async_copy(hid_oth.at[:, cols], mix, local_sem.at[0])]
            for move in moves:
                move.start()
            for move in moves:
                move.wait()

            @pl.loop(0, n_blocks)
            def _(i):
                here = pl.ds(pl.multiple_of(i * TOK, TOK), TOK)
                r0, r1 = take(1, i, segs, window)
                info, p = meta[1, here, :], probs[1, here, :]
                both = (lax.rem(info[:, 0:1], 2) == f) & (lax.rem(info[:, 1:2], 2) == f)
                whole = mix[here, :].astype(F32) + (p[:, 0:1] * r0 + p[:, 1:2] * r1)
                mix[here, :] = jnp.where(both, whole, r0 + r1).astype(BF16)

            moves = [pltpu.make_async_copy(mix.at[:, pl.ds(k * PIECE, PIECE)], y_own.at[chunk * pieces + k], local_sem.at[k]) for k in range(pieces)]
            for move in moves:
                move.start()
            for move in moves:
                move.wait()
            for k in range(pieces):
                y_copy(chunk * pieces + k).start()

        def final(half_id, step):
            q, k = lax.div(step, pieces), lax.rem(step, pieces)
            chunk = half_id * HALF_CHUNKS + q
            piece = chunk * pieces + k
            cols = pl.ds(pl.multiple_of(piece * PIECE, PIECE), PIECE)
            moves = fill(0, chunk, pl.ds(pl.multiple_of(k * PIECE, PIECE), PIECE), seg_piece) + [pltpu.make_async_copy(hid.at[:, cols], mix_piece, local_sem.at[0])]

            @pl.when(k == 0)
            def _():
                for r in (1, 2, 3):
                    back_copy(0, chunk, r).wait_recv()

            for move in moves:
                move.start()
            y_copy(piece).wait_recv()
            load = pltpu.make_async_copy(y_oth.at[piece], y_piece, local_sem.at[1])
            load.start()
            for move in moves:
                move.wait()
            load.wait()

            @pl.loop(0, n_blocks)
            def _(i):
                here = pl.ds(pl.multiple_of(i * TOK, TOK), TOK)
                r0, r1 = take(0, i, seg_piece, window_piece)
                info, p = meta[0, here, :], probs[0, here, :]
                near0, near1 = lax.rem(info[:, 0:1], 2) == f, lax.rem(info[:, 1:2], 2) == f
                far = y_piece[here, :].astype(F32)
                c0, c1 = jnp.where(near0, r0, far), jnp.where(near1, r1, far)
                whole = mix_piece[here, :].astype(F32) + (p[:, 0:1] * c0 + p[:, 1:2] * c1)
                mix_piece[here, :] = jnp.where(near0 | near1, whole, far).astype(BF16)

            store = pltpu.make_async_copy(mix_piece, out.at[:, cols], local_sem.at[0])
            store.start()
            store.wait()

        for s in range(2):
            @pl.loop(0, n_blocks)
            def _(i):
                shift = jnp.zeros_like(lane)
                for p in range(4):
                    shift = jnp.where(lane >= p * WINDOW, base_s[s, f * 4 + p, i] * 16 - p * WINDOW, shift)
                row = lane + shift
                info = meta[s, pl.ds(pl.multiple_of(i * TOK, TOK), TOK), :]
                for k in range(2):
                    picks[s, i, k * TOK:(k + 1) * TOK, :] = jnp.where(row == info[:, 2 + k:3 + k], 1.0, 0.0).astype(BF16)

        @pl.loop(0, HALF_CHUNKS)
        def _(q):
            expert_out(0, q)

        @pl.loop(0, HALF_CHUNKS)
        def _(q):
            expert_out(1, q)

            @pl.when(q == 0)
            def _():
                @pl.loop(0, HALF_CHUNKS)
                def _(z):
                    relay(f, z)

        @pl.loop(0, HALF_CHUNKS)
        def _(q):
            relay(1 - f, q)

        @pl.loop(0, 2 * HALF_CHUNKS * pieces)
        def _(step):
            late = lax.div(step, HALF_CHUNKS * pieces)
            final(jnp.where(late == 0, 1 - f, f), lax.rem(step, HALF_CHUNKS * pieces))

    pl.run_scoped(finish, pltpu.VMEM((2, n_blocks, 2 * TOK, 4 * WINDOW), BF16), pltpu.VMEM((4 * cap, dc), BF16), pltpu.VMEM((tok, dc), BF16),
                  pltpu.VMEM((4 * cap, PIECE), BF16), pltpu.VMEM((tok, PIECE), BF16), pltpu.VMEM((tok, PIECE), BF16),
                  pltpu.VMEM((4 * WINDOW, dc), BF16), pltpu.VMEM((4 * WINDOW, PIECE), BF16))

    ids_copy().wait_send()
    hid_copy().wait_send()
    for c in range(FF_CHUNKS):
        gate_copy(c).wait_send()
        up_copy(c).wait_send()
    for q in range(HALF_CHUNKS):
        down_copy(q).wait_send()
    for s in range(2):
        for r in (1, 2, 3):
            x_copy(s, r).wait_send()

    @pl.loop(0, chunks)
    def _(chunk):
        for s in range(2):
            for r in (1, 2, 3):
                back_copy(s, chunk, r).wait_send()
        for k in range(pieces):
            y_copy(chunk * pieces + k).wait_send()


def local_block(hidden, norm_gain, w_router, w_gate, w_up, w_down, top2_ids):
    tok, d_model = hidden.shape
    num_experts = w_router.shape[1]
    half, ff = w_gate.shape[1:]
    cap = (5 * tok + 2 * num_experts - 1) // (2 * num_experts)
    fc, dc = ff // FF_CHUNKS, half // HALF_CHUNKS
    n_rows = num_experts * cap
    shape = lambda *s: jax.ShapeDtypeStruct(s, BF16)
    dma = pltpu.SemaphoreType.DMA
    results = pl.pallas_call(
        functools.partial(moe_kernel, cap),
        out_shape=[shape(tok, d_model), shape(tok, d_model),
                   shape(FF_CHUNKS, half, fc), shape(FF_CHUNKS, half, fc), shape(HALF_CHUNKS, ff, dc),
                   shape(2, 4, cap, d_model), shape(n_rows, d_model), shape(n_rows, ff),
                   shape(2 * HALF_CHUNKS, n_rows, dc), shape(2, 2 * HALF_CHUNKS, 4 * cap, dc),
                   shape(d_model // PIECE, tok, PIECE), shape(d_model // PIECE, tok, PIECE)],
        in_specs=[ANY, VMEM, VMEM, VMEM, ANY, ANY, ANY],
        out_specs=[ANY] * 12,
        scratch_shapes=[
            pltpu.VMEM((num_experts, tok), jnp.int32), pltpu.VMEM((2, tok), jnp.int32),
            pltpu.VMEM((2, tok, 128), jnp.int32), pltpu.VMEM((2, tok, 128), F32), pltpu.VMEM((128, d_model), BF16),
            pltpu.VMEM((2, num_experts, TOK), jnp.int32), pltpu.SMEM((2, num_experts, TOK), jnp.int32),
            dma((6,)), dma((2, FF_CHUNKS)), dma((2, FF_CHUNKS)), dma((HALF_CHUNKS,)), dma((HALF_CHUNKS,)),
            dma((2,)), dma((2,)), dma((2, 4)), dma((2, 4)),
            dma((4 * HALF_CHUNKS, 4)), dma((4 * HALF_CHUNKS, 4)), dma((d_model // PIECE,)), dma((d_model // PIECE,))],
        compiler_params=pltpu.CompilerParams(collective_id=0, has_side_effects=True, vmem_limit_bytes=62 * 1024 * 1024),
    )(hidden, norm_gain, w_router.T, top2_ids.T, w_gate, w_up, w_down)
    return results[0]


def solution(mesh):
    tok_spec = P(('dp', 'fsdp', 'ep'), None)
    in_specs = (tok_spec, P(None), P(None, None), P('ep', 'fsdp', None), P('ep', 'fsdp', None), P('ep', None, 'fsdp'), tok_spec)
    return jax.shard_map(local_block, mesh=mesh, in_specs=in_specs, out_specs=tok_spec, check_vma=False)
```

time: 1350 us -> 1290 us (0.956)
  Pallas kernels: 1340 us -> 1280 us
    pallas_call x1, Pallas kernels: 1340 us -> 1280 us  [local_block(): pl.pallas_call(functools.partial(moe_kernel, cap), out_shape=[shape(tok,...]
where the time goes in v3:
time: 1290 us
  Pallas kernels  1280 us (99%)
    pallas_call x1, Pallas kernels, local_block(): pl.pallas_call(functools.partial(moe_kernel, cap), out_shape=[shape(tok,...  1280 us

profile of v3, /device:TPU:1, one launch (start us, length us, event | category | flops | bytes accessed | tf_op | source)
XLA Modules:
  0.0 1289.1 jit_solution(14664716699113648405)
XLA Ops:
  0.0 1281.1 %shard_map.73 = (bf16[2048,2304]{1,0:T(8,128)(2,1)}, bf16[2048,2304]{1,0:T(8,128)(2,1)}, bf16[5,1152,1152]{2,1,0:T(8,128)(2,1)}, bf16[5,1152,1152]{2,1,0:T(8,128...) custom-call(bf16[2048,2304]{1,0:T(8,128)(2,1)} %hid.1, ...), custom_call_target="tpu_custom_call" | custom-call | tf_op jit(solution)/shard_map/pallas_call | solution.py:388
  1281.1 8.0 copy.9

commit v4 on v3

--- a/solution.py
+++ b/solution.py
@@ -21,7 +21,7 @@
 
 
 def moe_kernel(cap, hid, gain, wr, ids, wg, wu, wd,
-               out, hid_oth, gate_in, up_in, down_in, x_send, x_all, h_all, o_all, back, y_own, y_oth,
+               out, y_oth, near, rule, hid_oth, gate_in, up_in, down_in, x_send, x_all, h_all, o_all, back, y_own,
                rows, ids_oth, meta, probs, wr_pad, base_v, base_s, local_sem, w_send, w_recv, d_send, d_recv,
                u_send, u_recv, x_ssem, x_rsem, b_send, b_recv, y_send, y_recv):
     tok, d_model = hid.shape
@@ -282,18 +282,28 @@
             for k in range(pieces):
                 y_copy(chunk * pieces + k).start()
 
-        def final(half_id, step):
-            q, k = lax.div(step, pieces), lax.rem(step, pieces)
+        def near_rows(half_id, q, k):
             chunk = half_id * HALF_CHUNKS + q
-            piece = chunk * pieces + k
-            cols = pl.ds(pl.multiple_of(piece * PIECE, PIECE), PIECE)
-            moves = fill(0, chunk, pl.ds(pl.multiple_of(k * PIECE, PIECE), PIECE), seg_piece) + [pltpu.make_async_copy(hid.at[:, cols], mix_piece, local_sem.at[0])]
 
             @pl.when(k == 0)
             def _():
                 for r in (1, 2, 3):
                     back_copy(0, chunk, r).wait_recv()
 
+            return fill(0, chunk, pl.ds(pl.multiple_of(k * PIECE, PIECE), PIECE), seg_piece)
+
+        def near_far(i):
+            here = pl.ds(pl.multiple_of(i * TOK, TOK), TOK)
+            r0, r1 = take(0, i, seg_piece, window_piece)
+            info, p = meta[0, here, :], probs[0, here, :]
+            near0, near1 = lax.rem(info[:, 0:1], 2) == f, lax.rem(info[:, 1:2], 2) == f
+            return here, r0, r1, near0, near1, p[:, 0:1], p[:, 1:2]
+
+        def final(half_id, step):
+            q, k = lax.div(step, pieces), lax.rem(step, pieces)
+            piece = (half_id * HALF_CHUNKS + q) * pieces + k
+            cols = pl.ds(pl.multiple_of(piece * PIECE, PIECE), PIECE)
+            moves = near_rows(half_id, q, k) + [pltpu.make_async_copy(hid.at[:, cols], mix_piece, local_sem.at[0])]
             for move in moves:
                 move.start()
             y_copy(piece).wait_recv()
@@ -305,18 +315,39 @@
 
             @pl.loop(0, n_blocks)
             def _(i):
-                here = pl.ds(pl.multiple_of(i * TOK, TOK), TOK)
-                r0, r1 = take(0, i, seg_piece, window_piece)
-                info, p = meta[0, here, :], probs[0, here, :]
-                near0, near1 = lax.rem(info[:, 0:1], 2) == f, lax.rem(info[:, 1:2], 2) == f
+                here, r0, r1, near0, near1, p0, p1 = near_far(i)
                 far = y_piece[here, :].astype(F32)
                 c0, c1 = jnp.where(near0, r0, far), jnp.where(near1, r1, far)
-                whole = mix_piece[here, :].astype(F32) + (p[:, 0:1] * c0 + p[:, 1:2] * c1)
+                whole = mix_piece[here, :].astype(F32) + (p0 * c0 + p1 * c1)
                 mix_piece[here, :] = jnp.where(near0 | near1, whole, far).astype(BF16)
 
             store = pltpu.make_async_copy(mix_piece, out.at[:, cols], local_sem.at[0])
             store.start()
             store.wait()
+
+        def leave_last(near_buf, rule_buf):
+            last = HALF_CHUNKS * pieces - 1
+            moves = near_rows(f, last // pieces, last % pieces)
+            for move in moves:
+                move.start()
+            for move in moves:
+                move.wait()
+            lanes = lax.broadcasted_iota(jnp.int32, (TOK, PIECE), 1)
+
+            @pl.loop(0, n_blocks)
+            def _(i):
+                here, r0, r1, near0, near1, p0, p1 = near_far(i)
+                near_buf[here, :] = p0 * jnp.where(near0, r0, 0.0) + p1 * jnp.where(near1, r1, 0.0)
+                p_far = jnp.where(near0, jnp.where(near1, 0.0, p1), p0)
+                all_far = jnp.where(near0 | near1, 0.0, 1.0)
+                rule_buf[here, :] = jnp.where(lanes == 0, p_far, all_far)
+
+            moves = [pltpu.make_async_copy(near_buf, near, local_sem.at[0]), pltpu.make_async_copy(rule_buf, rule, local_sem.at[1])]
+            for move in moves:
+                move.start()
+            for move in moves:
+                move.wait()
+            y_copy(f * HALF_CHUNKS * pieces + last).wait_recv()
 
         for s in range(2):
             @pl.loop(0, n_blocks)
@@ -347,10 +378,12 @@
         def _(q):
             relay(1 - f, q)
 
-        @pl.loop(0, 2 * HALF_CHUNKS * pieces)
+        @pl.loop(0, 2 * HALF_CHUNKS * pieces - 1)
         def _(step):
             late = lax.div(step, HALF_CHUNKS * pieces)
             final(jnp.where(late == 0, 1 - f, f), lax.rem(step, HALF_CHUNKS * pieces))
+
+        pl.run_scoped(leave_last, pltpu.VMEM((tok, PIECE), F32), pltpu.VMEM((tok, PIECE), F32))
 
     pl.run_scoped(finish, pltpu.VMEM((2, n_blocks, 2 * TOK, 4 * WINDOW), BF16), pltpu.VMEM((4 * cap, dc), BF16), pltpu.VMEM((tok, dc), BF16),
                   pltpu.VMEM((4 * cap, PIECE), BF16), pltpu.VMEM((tok, PIECE), BF16), pltpu.VMEM((tok, PIECE), BF16),
@@ -374,6 +407,29 @@
                 back_copy(s, chunk, r).wait_send()
         for k in range(pieces):
             y_copy(chunk * pieces + k).wait_send()
+
+
+def last_piece_kernel(part, y_oth, near, rule, hid, out):
+    tok, d_model = part.shape
+    half = d_model // 2
+    piece = (lax.axis_index('fsdp') + 1) * (half // PIECE) - 1
+    cols = pl.ds(pl.multiple_of(piece * PIECE, PIECE), PIECE)
+
+    def body(part_ref, y_ref, near_ref, rule_ref, hid_ref, out_ref):
+        out_ref[...] = part_ref[...]
+        far = y_ref[...].astype(F32)
+        p_far, all_far = rule_ref[:, 0:1], rule_ref[:, 1:2]
+        whole = hid_ref[...].astype(F32) + (near_ref[...] + p_far * far)
+        out_ref[:, cols] = jnp.where(all_far > 0.0, far, whole).astype(BF16)
+
+    block = 128
+    narrow = pl.BlockSpec((block, PIECE), lambda i: (i, 0))
+    wide = pl.BlockSpec((block, d_model), lambda i: (i, 0))
+    pltpu.emit_pipeline(
+        body, grid=(tok // block,),
+        in_specs=[wide, narrow, narrow, narrow, pl.BlockSpec((block, PIECE), lambda i: (i, piece))],
+        out_specs=[wide],
+    )(part, y_oth.at[piece], near, rule, hid, out)
 
 
 def local_block(hidden, norm_gain, w_router, w_gate, w_up, w_down, top2_ids):
@@ -387,13 +443,14 @@
     dma = pltpu.SemaphoreType.DMA
     results = pl.pallas_call(
         functools.partial(moe_kernel, cap),
-        out_shape=[shape(tok, d_model), shape(tok, d_model),
+        out_shape=[shape(tok, d_model), shape(d_model // PIECE, tok, PIECE),
+                   jax.ShapeDtypeStruct((tok, PIECE), F32), jax.ShapeDtypeStruct((tok, PIECE), F32), shape(tok, d_model),
                    shape(FF_CHUNKS, half, fc), shape(FF_CHUNKS, half, fc), shape(HALF_CHUNKS, ff, dc),
                    shape(2, 4, cap, d_model), shape(n_rows, d_model), shape(n_rows, ff),
                    shape(2 * HALF_CHUNKS, n_rows, dc), shape(2, 2 * HALF_CHUNKS, 4 * cap, dc),
-                   shape(d_model // PIECE, tok, PIECE), shape(d_model // PIECE, tok, PIECE)],
+                   shape(d_model // PIECE, tok, PIECE)],
         in_specs=[ANY, VMEM, VMEM, VMEM, ANY, ANY, ANY],
-        out_specs=[ANY] * 12,
+        out_specs=[ANY] * 14,
         scratch_shapes=[
             pltpu.VMEM((num_experts, tok), jnp.int32), pltpu.VMEM((2, tok), jnp.int32),
             pltpu.VMEM((2, tok, 128), jnp.int32), pltpu.VMEM((2, tok, 128), F32), pltpu.VMEM((128, d_model), BF16),
@@ -403,7 +460,10 @@
             dma((4 * HALF_CHUNKS, 4)), dma((4 * HALF_CHUNKS, 4)), dma((d_model // PIECE,)), dma((d_model // PIECE,))],
         compiler_params=pltpu.CompilerParams(collective_id=0, has_side_effects=True, vmem_limit_bytes=62 * 1024 * 1024),
     )(hidden, norm_gain, w_router.T, top2_ids.T, w_gate, w_up, w_down)
-    return results[0]
+    return pl.pallas_call(
+        last_piece_kernel, out_shape=shape(tok, d_model), in_specs=[ANY] * 5, out_specs=ANY,
+        compiler_params=pltpu.CompilerParams(vmem_limit_bytes=62 * 1024 * 1024),
+    )(*results[:4], hidden)
 
 
 def solution(mesh):

time: 1290 us -> 1300 us (level)
  Pallas kernels: 1280 us -> 1300 us
    pallas_call x0 -> x1, Pallas kernels: none -> 13.5 us  [local_block(): pl.pallas_call(last_piece_kernel, out_shape=shape(tok, d_model), in_specs...]
where the time goes in v4:
time: 1300 us
  Pallas kernels  1300 us (100%)
    pallas_call x1, Pallas kernels, local_block(): pl.pallas_call(functools.partial(moe_kernel, cap), out_shape=[shape(tok,...  1280 us

profile of v4, /device:TPU:1, one launch (start us, length us, event | category | flops | bytes accessed | tf_op | source)
XLA Modules:
  0.0 1297.4 jit_solution(15451978499866888397)
XLA Ops:
  0.0 1284.0 %shard_map.73 = (bf16[2048,2304]{1,0:T(8,128)(2,1)}, bf16[18,2048,128]{2,1,0:T(8,128)(2,1)}, f32[2048,128]{1,0:T(8,128)}, f32[2048,128]{1,0:T(8,128)}, bf16[2048...) custom-call(bf16[2048,2304]{1,0:T(8,128)(2,1)} %hid.3, ...), custom_call_target="tpu_custom_call" | custom-call | tf_op jit(solution)/shard_map/pallas_call | solution.py:444
  1284.0 13.5 %shard_map.74 = bf16[2048,2304]{1,0:T(8,128)(2,1)} custom-call(bf16[2048,2304]{1,0:T(8,128)(2,1)} %get-tuple-element.9.part, bf16[18,2048,128]{2,1,0:T(8,128)(2,1)} %get-tuple-element.10.y_oth, f32[2048,128]{1,0:T(8,128)} %get-tuple-element.11.near, f32[2048,128]{1,0:T(8,128)} %get-tuple-element.12.rule, bf16[2048,2304]{1,0:T(8,128)(2,1)} %hid.3), custom_call_target="tpu_custom_call" | custom-call | tf_op jit(solution)/shard_map/pallas_call | solution.py:463

commit v5 on v3

--- a/solution.py
+++ b/solution.py
@@ -23,7 +23,7 @@
 def moe_kernel(cap, hid, gain, wr, ids, wg, wu, wd,
                out, hid_oth, gate_in, up_in, down_in, x_send, x_all, h_all, o_all, back, y_own, y_oth,
                rows, ids_oth, meta, probs, wr_pad, base_v, base_s, local_sem, w_send, w_recv, d_send, d_recv,
-               u_send, u_recv, x_ssem, x_rsem, b_send, b_recv, y_send, y_recv):
+               u_send, u_recv, x_ssem, x_rsem, b_send, b_recv, y_send, y_recv, y_sem):
     tok, d_model = hid.shape
     half = d_model // 2
     ff = wg.shape[2]
@@ -220,7 +220,7 @@
             here = pl.ds(pl.multiple_of(i * sub, sub), sub)
             o_ref[here, :] = jnp.dot(h_ref[here, :], w_ref[...], preferred_element_type=F32).astype(BF16)
 
-    def finish(picks, segs, mix, seg_piece, mix_piece, y_piece, window, window_piece):
+    def finish(picks, segs, mix, y_buf, window, window_piece):
         side_rows = 4 * WINDOW
         lane = lax.broadcasted_iota(jnp.int32, (1, side_rows), 1)
 
@@ -282,41 +282,71 @@
             for k in range(pieces):
                 y_copy(chunk * pieces + k).start()
 
-        def final(half_id, step):
-            q, k = lax.div(step, pieces), lax.rem(step, pieces)
+        def near_copies(chunk):
+            cols = pl.ds(pl.multiple_of(chunk * dc, PIECE), dc)
+            return fill(0, chunk, pl.ds(0, dc), segs) + [pltpu.make_async_copy(hid.at[:, cols], mix, local_sem.at[0])]
+
+        def start_near(chunk):
+            for r in (1, 2, 3):
+                back_copy(0, chunk, r).wait_recv()
+            for move in near_copies(chunk):
+                move.start()
+
+        def settle(here, r0, r1, k):
+            info, p = meta[0, here, :], probs[0, here, :]
+            near0, near1 = lax.rem(info[:, 0:1], 2) == f, lax.rem(info[:, 1:2], 2) == f
+            cols = slice(k * PIECE, (k + 1) * PIECE)
+            far = y_buf[k, here, :].astype(F32)
+            c0, c1 = jnp.where(near0, r0, far), jnp.where(near1, r1, far)
+            whole = mix[here, cols].astype(F32) + (p[:, 0:1] * c0 + p[:, 1:2] * c1)
+            mix[here, cols] = jnp.where(near0 | near1, whole, far).astype(BF16)
+
+        def final(half_id, q):
             chunk = half_id * HALF_CHUNKS + q
-            piece = chunk * pieces + k
-            cols = pl.ds(pl.multiple_of(piece * PIECE, PIECE), PIECE)
-            moves = fill(0, chunk, pl.ds(pl.multiple_of(k * PIECE, PIECE), PIECE), seg_piece) + [pltpu.make_async_copy(hid.at[:, cols], mix_piece, local_sem.at[0])]
-
-            @pl.when(k == 0)
-            def _():
-                for r in (1, 2, 3):
-                    back_copy(0, chunk, r).wait_recv()
-
-            for move in moves:
-                move.start()
-            y_copy(piece).wait_recv()
-            load = pltpu.make_async_copy(y_oth.at[piece], y_piece, local_sem.at[1])
-            load.start()
-            for move in moves:
+            cols = pl.ds(pl.multiple_of(chunk * dc, PIECE), dc)
+            start_near(chunk)
+            loads = [pltpu.make_async_copy(y_oth.at[chunk * pieces + k], y_buf.at[k], y_sem.at[k]) for k in range(pieces)]
+            for k in range(pieces):
+                y_copy(chunk * pieces + k).wait_recv()
+                loads[k].start()
+            for move in near_copies(chunk) + loads:
                 move.wait()
-            load.wait()
 
             @pl.loop(0, n_blocks)
             def _(i):
                 here = pl.ds(pl.multiple_of(i * TOK, TOK), TOK)
-                r0, r1 = take(0, i, seg_piece, window_piece)
-                info, p = meta[0, here, :], probs[0, here, :]
-                near0, near1 = lax.rem(info[:, 0:1], 2) == f, lax.rem(info[:, 1:2], 2) == f
-                far = y_piece[here, :].astype(F32)
-                c0, c1 = jnp.where(near0, r0, far), jnp.where(near1, r1, far)
-                whole = mix_piece[here, :].astype(F32) + (p[:, 0:1] * c0 + p[:, 1:2] * c1)
-                mix_piece[here, :] = jnp.where(near0 | near1, whole, far).astype(BF16)
-
-            store = pltpu.make_async_copy(mix_piece, out.at[:, cols], local_sem.at[0])
+                r0, r1 = take(0, i, segs, window)
+                for k in range(pieces):
+                    settle(here, r0[:, k * PIECE:(k + 1) * PIECE], r1[:, k * PIECE:(k + 1) * PIECE], k)
+
+            store = pltpu.make_async_copy(mix, out.at[:, cols], local_sem.at[0])
             store.start()
             store.wait()
+
+        def final_last():
+            chunk = f * HALF_CHUNKS + HALF_CHUNKS - 1
+            start_near(chunk)
+            for move in near_copies(chunk):
+                move.wait()
+            stores = []
+            for k in range(pieces):
+                piece = chunk * pieces + k
+                y_copy(piece).wait_recv()
+                load = pltpu.make_async_copy(y_oth.at[piece], y_buf.at[k], y_sem.at[k])
+                load.start()
+                load.wait()
+
+                @pl.loop(0, n_blocks)
+                def _(i):
+                    here = pl.ds(pl.multiple_of(i * TOK, TOK), TOK)
+                    r0, r1 = take(0, i, segs.at[:, pl.ds(k * PIECE, PIECE)], window_piece)
+                    settle(here, r0, r1, k)
+
+                stores.append(pltpu.make_async_copy(mix.at[:, pl.ds(k * PIECE, PIECE)],
+                                                    out.at[:, pl.ds(pl.multiple_of(piece * PIECE, PIECE), PIECE)], y_sem.at[k]))
+                stores[k].start()
+            for store in stores:
+                store.wait()
 
         for s in range(2):
             @pl.loop(0, n_blocks)
@@ -347,13 +377,14 @@
         def _(q):
             relay(1 - f, q)
 
-        @pl.loop(0, 2 * HALF_CHUNKS * pieces)
+        @pl.loop(0, 2 * HALF_CHUNKS - 1)
         def _(step):
-            late = lax.div(step, HALF_CHUNKS * pieces)
-            final(jnp.where(late == 0, 1 - f, f), lax.rem(step, HALF_CHUNKS * pieces))
+            final(jnp.where(step < HALF_CHUNKS, 1 - f, f), lax.rem(step, HALF_CHUNKS))
+
+        final_last()
 
     pl.run_scoped(finish, pltpu.VMEM((2, n_blocks, 2 * TOK, 4 * WINDOW), BF16), pltpu.VMEM((4 * cap, dc), BF16), pltpu.VMEM((tok, dc), BF16),
-                  pltpu.VMEM((4 * cap, PIECE), BF16), pltpu.VMEM((tok, PIECE), BF16), pltpu.VMEM((tok, PIECE), BF16),
+                  pltpu.VMEM((pieces, tok, PIECE), BF16),
                   pltpu.VMEM((4 * WINDOW, dc), BF16), pltpu.VMEM((4 * WINDOW, PIECE), BF16))
 
     ids_copy().wait_send()
@@ -400,7 +431,7 @@
             pltpu.VMEM((2, num_experts, TOK), jnp.int32), pltpu.SMEM((2, num_experts, TOK), jnp.int32),
             dma((6,)), dma((2, FF_CHUNKS)), dma((2, FF_CHUNKS)), dma((HALF_CHUNKS,)), dma((HALF_CHUNKS,)),
             dma((2,)), dma((2,)), dma((2, 4)), dma((2, 4)),
-            dma((4 * HALF_CHUNKS, 4)), dma((4 * HALF_CHUNKS, 4)), dma((d_model // PIECE,)), dma((d_model // PIECE,))],
+            dma((4 * HALF_CHUNKS, 4)), dma((4 * HALF_CHUNKS, 4)), dma((d_model // PIECE,)), dma((d_model // PIECE,)), dma((half // HALF_CHUNKS // PIECE,))],
         compiler_params=pltpu.CompilerParams(collective_id=0, has_side_effects=True, vmem_limit_bytes=62 * 1024 * 1024),
     )(hidden, norm_gain, w_router.T, top2_ids.T, w_gate, w_up, w_down)
     return results[0]

time: 1290 us -> 1280 us (level)
  no operation moved by 1% of the time
where the time goes in v5:
time: 1280 us
  Pallas kernels  1270 us (99%)
    pallas_call x1, Pallas kernels, local_block(): pl.pallas_call(functools.partial(moe_kernel, cap), out_shape=[shape(tok,...  1270 us

profile of v5, /device:TPU:1, one launch (start us, length us, event | category | flops | bytes accessed | tf_op | source)
XLA Modules:
  0.0 1279.3 jit_solution(14735120951689187977)
XLA Ops:
  0.0 1271.3 %shard_map.73 = (bf16[2048,2304]{1,0:T(8,128)(2,1)}, bf16[2048,2304]{1,0:T(8,128)(2,1)}, bf16[5,1152,1152]{2,1,0:T(8,128)(2,1)}, bf16[5,1152,1152]{2,1,0:T(8,128...) custom-call(bf16[2048,2304]{1,0:T(8,128)(2,1)} %hid.1, ...), custom_call_target="tpu_custom_call" | custom-call | tf_op jit(solution)/shard_map/pallas_call | solution.py:419
  1271.3 8.0 copy.9

commit v6 on v5

--- a/solution.py
+++ b/solution.py
@@ -16,6 +16,7 @@
 FF_CHUNKS = 5
 HALF_CHUNKS = 3
 PIECE = 128
+PARTS = 2
 TOK = 128
 WINDOW = TOK + 16
 
@@ -75,8 +76,9 @@
         return remote(o_all.at[chunk, pl.ds(owner * cap, cap)], back.at[s, chunk, pl.ds(j * cap, cap)],
                       b_send.at[s * chunks + chunk, r], b_recv.at[s * chunks + chunk, r], r)
 
-    def y_copy(piece):
-        return remote(y_own.at[piece], y_oth.at[piece], y_send.at[piece], y_recv.at[piece], 4)
+    def y_copy(piece, part):
+        here = pl.ds(part * (tok // PARTS), tok // PARTS)
+        return remote(y_own.at[piece, here], y_oth.at[piece, here], y_send.at[piece, part], y_recv.at[piece, part], 4)
 
     barrier = pltpu.get_barrier_semaphore()
     for r in range(1, n_dev):
@@ -220,7 +222,7 @@
             here = pl.ds(pl.multiple_of(i * sub, sub), sub)
             o_ref[here, :] = jnp.dot(h_ref[here, :], w_ref[...], preferred_element_type=F32).astype(BF16)
 
-    def finish(picks, segs, mix, y_buf, window, window_piece):
+    def finish(picks, segs, mix, y_buf, window, near):
         side_rows = 4 * WINDOW
         lane = lax.broadcasted_iota(jnp.int32, (1, side_rows), 1)
 
@@ -280,7 +282,8 @@
             for move in moves:
                 move.wait()
             for k in range(pieces):
-                y_copy(chunk * pieces + k).start()
+                for part in range(PARTS):
+                    y_copy(chunk * pieces + k, part).start()
 
         def near_copies(chunk):
             cols = pl.ds(pl.multiple_of(chunk * dc, PIECE), dc)
@@ -305,9 +308,10 @@
             chunk = half_id * HALF_CHUNKS + q
             cols = pl.ds(pl.multiple_of(chunk * dc, PIECE), dc)
             start_near(chunk)
-            loads = [pltpu.make_async_copy(y_oth.at[chunk * pieces + k], y_buf.at[k], y_sem.at[k]) for k in range(pieces)]
+            loads = [pltpu.make_async_copy(y_oth.at[chunk * pieces + k], y_buf.at[k], y_sem.at[k, 0]) for k in range(pieces)]
             for k in range(pieces):
-                y_copy(chunk * pieces + k).wait_recv()
+                for part in range(PARTS):
+                    y_copy(chunk * pieces + k, part).wait_recv()
                 loads[k].start()
             for move in near_copies(chunk) + loads:
                 move.wait()
@@ -328,23 +332,41 @@
             start_near(chunk)
             for move in near_copies(chunk):
                 move.wait()
+
+            @pl.loop(0, n_blocks)
+            def _(i):
+                here = pl.ds(pl.multiple_of(i * TOK, TOK), TOK)
+                r0, r1 = take(0, i, segs, window)
+                info, p = meta[0, here, :], probs[0, here, :]
+                near0, near1 = lax.rem(info[:, 0:1], 2) == f, lax.rem(info[:, 1:2], 2) == f
+                near[here, :] = p[:, 0:1] * jnp.where(near0, r0, 0.0) + p[:, 1:2] * jnp.where(near1, r1, 0.0)
+
             stores = []
+            part_rows = tok // PARTS
             for k in range(pieces):
-                piece = chunk * pieces + k
-                y_copy(piece).wait_recv()
-                load = pltpu.make_async_copy(y_oth.at[piece], y_buf.at[k], y_sem.at[k])
-                load.start()
-                load.wait()
-
-                @pl.loop(0, n_blocks)
-                def _(i):
-                    here = pl.ds(pl.multiple_of(i * TOK, TOK), TOK)
-                    r0, r1 = take(0, i, segs.at[:, pl.ds(k * PIECE, PIECE)], window_piece)
-                    settle(here, r0, r1, k)
-
-                stores.append(pltpu.make_async_copy(mix.at[:, pl.ds(k * PIECE, PIECE)],
-                                                    out.at[:, pl.ds(pl.multiple_of(piece * PIECE, PIECE), PIECE)], y_sem.at[k]))
-                stores[k].start()
+                for part in range(PARTS):
+                    piece = chunk * pieces + k
+                    rows_here = pl.ds(part * part_rows, part_rows)
+                    y_copy(piece, part).wait_recv()
+                    load = pltpu.make_async_copy(y_oth.at[piece, rows_here], y_buf.at[k, rows_here], y_sem.at[k, part])
+                    load.start()
+                    load.wait()
+                    cols = slice(k * PIECE, (k + 1) * PIECE)
+
+                    @pl.loop(part * (n_blocks // PARTS), (part + 1) * (n_blocks // PARTS))
+                    def _(i):
+                        here = pl.ds(pl.multiple_of(i * TOK, TOK), TOK)
+                        info, p = meta[0, here, :], probs[0, here, :]
+                        near0, near1 = lax.rem(info[:, 0:1], 2) == f, lax.rem(info[:, 1:2], 2) == f
+                        p_far = jnp.where(near0, jnp.where(near1, 0.0, p[:, 1:2]), p[:, 0:1])
+                        far = y_buf[k, here, :].astype(F32)
+                        whole = mix[here, cols].astype(F32) + (near[here, cols] + p_far * far)
+                        mix[here, cols] = jnp.where(near0 | near1, whole, far).astype(BF16)
+
+                    store = pltpu.make_async_copy(mix.at[rows_here, pl.ds(k * PIECE, PIECE)],
+                                                  out.at[rows_here, pl.ds(pl.multiple_of(piece * PIECE, PIECE), PIECE)], y_sem.at[k, part])
+                    store.start()
+                    stores.append(store)
             for store in stores:
                 store.wait()
 
@@ -385,7 +407,7 @@
 
     pl.run_scoped(finish, pltpu.VMEM((2, n_blocks, 2 * TOK, 4 * WINDOW), BF16), pltpu.VMEM((4 * cap, dc), BF16), pltpu.VMEM((tok, dc), BF16),
                   pltpu.VMEM((pieces, tok, PIECE), BF16),
-                  pltpu.VMEM((4 * WINDOW, dc), BF16), pltpu.VMEM((4 * WINDOW, PIECE), BF16))
+                  pltpu.VMEM((4 * WINDOW, dc), BF16), pltpu.VMEM((tok, dc), F32))
 
     ids_copy().wait_send()
     hid_copy().wait_send()
@@ -404,7 +426,8 @@
             for r in (1, 2, 3):
                 back_copy(s, chunk, r).wait_send()
         for k in range(pieces):
-            y_copy(chunk * pieces + k).wait_send()
+            for part in range(PARTS):
+                y_copy(chunk * pieces + k, part).wait_send()
 
 
 def local_block(hidden, norm_gain, w_router, w_gate, w_up, w_down, top2_ids):
@@ -431,7 +454,7 @@
             pltpu.VMEM((2, num_experts, TOK), jnp.int32), pltpu.SMEM((2, num_experts, TOK), jnp.int32),
             dma((6,)), dma((2, FF_CHUNKS)), dma((2, FF_CHUNKS)), dma((HALF_CHUNKS,)), dma((HALF_CHUNKS,)),
             dma((2,)), dma((2,)), dma((2, 4)), dma((2, 4)),
-            dma((4 * HALF_CHUNKS, 4)), dma((4 * HALF_CHUNKS, 4)), dma((d_model // PIECE,)), dma((d_model // PIECE,)), dma((half // HALF_CHUNKS // PIECE,))],
+            dma((4 * HALF_CHUNKS, 4)), dma((4 * HALF_CHUNKS, 4)), dma((d_model // PIECE, PARTS)), dma((d_model // PIECE, PARTS)), dma((half // HALF_CHUNKS // PIECE, PARTS))],
         compiler_params=pltpu.CompilerParams(collective_id=0, has_side_effects=True, vmem_limit_bytes=62 * 1024 * 1024),
     )(hidden, norm_gain, w_router.T, top2_ids.T, w_gate, w_up, w_down)
     return results[0]

time: 1280 us -> 1280 us (level)
  no operation moved by 1% of the time
where the time goes in v6:
time: 1280 us
  Pallas kernels  1270 us (99%)
    pallas_call x1, Pallas kernels, local_block(): pl.pallas_call(functools.partial(moe_kernel, cap), out_shape=[shape(tok,...  1270 us

profile of v6, /device:TPU:1, one launch (start us, length us, event | category | flops | bytes accessed | tf_op | source)
XLA Modules:
  0.0 1276.7 jit_solution(16853524019557229095)
XLA Ops:
  0.0 1268.7 %shard_map.73 = (bf16[2048,2304]{1,0:T(8,128)(2,1)}, bf16[2048,2304]{1,0:T(8,128)(2,1)}, bf16[5,1152,1152]{2,1,0:T(8,128)(2,1)}, bf16[5,1152,1152]{2,1,0:T(8,128...) custom-call(bf16[2048,2304]{1,0:T(8,128)(2,1)} %hid.1, ...), custom_call_target="tpu_custom_call" | custom-call | tf_op jit(solution)/shard_map/pallas_call | solution.py:442
  1268.7 8.0 copy.9
